TPU v7x, 32 devices: a whole 2x2x4 slice. The times are simulated.
32 devices in a mesh: row: 8 (over y, x, core), col: 4 (over z).
Axes of the slice: x: 2, y: 2, z: 4, core: 2. Of those that a mesh axis runs over, the one named last changes fastest.
Arguments:
- covariance: bfloat16 [16384, 16384], P('row', 'col'), may hold values from -0.12 to 0.6, as said below
- estimate: bfloat16 [16384, 16384], P('row', 'col'), may hold values from -2.3 to 12, as said below
- dual_var: bfloat16 [16384, 16384], P('row', 'col'), may hold values from -1.7 to 1.7, as said below
- start_basis: float32 [16384, 128], P('row'), may hold values from -6 to 6
Outputs:
- next_estimate: float32 [16384, 16384], P('row', 'col')
- next_dual: bfloat16 [16384, 16384], P('row', 'col')
Inputs may be any that keep to these rules, and one draw needn't show every extreme that they name: `covariance`: symmetric. `estimate`: symmetric. `dual_var`: symmetric.
All inputs are finite; a program needn't handle non-finite values.
Results may differ from a plain program's by a relative error of at most 0.001.
Values sent between devices are 32-bit elements; how exact they have to be, the bound alone decides.
No kernel may reach another device: no remote copies, remote signals or barrier semaphores. Data moves between devices by JAX's collectives and lax.ppermute only.
A program may use at most 192 MiB of HBM per device.

v0:
```python
import functools

import jax
import jax.numpy as jnp
from jax import lax
from jax.experimental import pallas as pl
from jax.experimental.pallas import tpu as pltpu
from jax.sharding import PartitionSpec as P


NS_ITERS = 12


penalty = 0.01
threshold = 0.2
base_level = 10.0
highest = lax.Precision.HIGHEST


def from_root(value, axis, source):
    kept = jnp.where(lax.axis_index(axis) == source, value, 0).astype(value.dtype)
    return lax.psum(kept, axis)


def inner_product(left_side, right_side):
    return lax.dot_general(
        left_side,
        right_side,
        (((0,), (0,)), ((), ())),
        precision=highest,
        preferred_element_type=jnp.float32,
    )


def normalize(mapped, gram_matrix):
    lower_factor = jnp.linalg.cholesky(gram_matrix)
    identity = jnp.eye(gram_matrix.shape[0], dtype=jnp.float32)
    inverse = lax.linalg.triangular_solve(lower_factor, identity, left_side=True, lower=True)
    return jnp.dot(mapped, inverse.T, precision=highest, preferred_element_type=jnp.float32)


def response_of(ritz_matrix):
    identity = jnp.eye(ritz_matrix.shape[0], dtype=jnp.float32)
    square = (
        jnp.dot(ritz_matrix, ritz_matrix, precision=highest, preferred_element_type=jnp.float32)
        + 4.0 * penalty * identity
    )
    frobenius = jnp.sqrt(jnp.sum(square * square))

    def newton(sweep_index, state_pair):
        iterate, partner = state_pair
        factor = 0.5 * (
            3.0 * identity
            - jnp.dot(partner, iterate, precision=highest, preferred_element_type=jnp.float32)
        )
        return (
            jnp.dot(iterate, factor, precision=highest, preferred_element_type=jnp.float32),
            jnp.dot(factor, partner, precision=highest, preferred_element_type=jnp.float32),
        )

    iterate, _ = lax.fori_loop(0, NS_ITERS, newton, (square / frobenius, identity))
    square_root = jnp.sqrt(frobenius) * iterate
    return (ritz_matrix + square_root) / (2.0 * penalty) - base_level * identity


def column_basis(shifted, row_basis):
    partial_terms = lax.dot_general(
        shifted,
        row_basis,
        (((0,), (0,)), ((), ())),
        precision=highest,
        preferred_element_type=jnp.float32,
    )
    mapped = lax.psum(partial_terms, "row")
    gram_matrix = lax.psum(inner_product(mapped, mapped), "col")
    return normalize(mapped, gram_matrix)


def row_image(shifted, col_basis):
    local_terms = jnp.dot(shifted, col_basis, precision=highest, preferred_element_type=jnp.float32)
    return lax.psum(local_terms, "col")


def row_inner(left_side, right_side):
    return lax.psum(inner_product(left_side, right_side), "row")


def body(covariance, estimate, dual_var, start_basis):
    shifted = penalty * (
        estimate.astype(jnp.float32) - dual_var.astype(jnp.float32)
    ) - covariance.astype(jnp.float32)
    rows_tile = shifted.shape[0]
    cols_tile = shifted.shape[1]
    row_basis = start_basis
    col_basis = column_basis(shifted, row_basis)
    blocks_per_column = lax.axis_size("row") // lax.axis_size("col")
    row_index = lax.axis_index("row")
    own_block = lax.dynamic_slice_in_dim(
        col_basis, row_index % blocks_per_column * rows_tile, rows_tile, 0
    )
    row_basis = from_root(own_block, "col", row_index // blocks_per_column)
    product = row_image(shifted, col_basis)
    raw_ritz = row_inner(row_basis, product)
    ritz_matrix = 0.5 * (raw_ritz + raw_ritz.T)
    response = response_of(ritz_matrix)
    weighted = jnp.dot(row_basis, response, precision=highest, preferred_element_type=jnp.float32)
    theta_tile = lax.dot_general(
        weighted,
        col_basis,
        (((1,), (1,)), ((), ())),
        precision=highest,
        preferred_element_type=jnp.float32,
    )
    row_ids = row_index * rows_tile + lax.broadcasted_iota(jnp.int32, (rows_tile, 1), 0)
    col_ids = lax.axis_index("col") * cols_tile + lax.broadcasted_iota(jnp.int32, (1, cols_tile), 1)
    theta_tile = theta_tile + jnp.where(row_ids == col_ids, base_level, 0.0)
    mixture = theta_tile + dual_var.astype(jnp.float32)
    clipped = jnp.clip(mixture, -threshold, threshold)
    return (mixture - clipped, clipped.astype(jnp.bfloat16))


def in_hbm(value):
    return pltpu.with_memory_space_constraint(value, pltpu.HBM)


def in_vmem(value):
    return pltpu.with_memory_space_constraint(value, pltpu.VMEM)


def split_two(value):
    high = value.astype(jnp.bfloat16)
    low = (value - high.astype(jnp.float32)).astype(jnp.bfloat16)
    return high, low


def contract(left_side, right_side, dims):
    return lax.dot_general(
        left_side, right_side, (dims, ((), ())), preferred_element_type=jnp.float32
    )


def image_kernel(order_ref, est_ref, dual_ref, cov_ref, basis_ref, *refs):
    part_ref, high_ref, held_ref, *more = refs
    step = pl.program_id(0)
    rows, width = est_ref.shape
    rank = part_ref.shape[1]
    stack_ref = basis_ref
    if more:
        stack_ref = more[0]

        @pl.when(step == 0)
        def _():
            high, low = split_two(basis_ref[...].T)
            stack_ref[:rank, :] = high
            stack_ref[rank:, :] = low

    depth = min(rows, 512)
    total = jnp.zeros((2 * rank, width), jnp.float32)
    extra = jnp.zeros((rank, width), jnp.float32)
    columns = pl.ds(pl.multiple_of(step * width, width), width)
    for start in range(0, rows, depth):
        span = slice(start, start + depth)
        dual_piece = dual_ref[span, :]
        shifted = penalty * (
            est_ref[span, :].astype(jnp.float32) - dual_piece.astype(jnp.float32)
        ) - cov_ref[span, :].astype(jnp.float32)
        high, low = split_two(shifted)
        high_ref[span, columns] = high
        held_ref[span, columns] = dual_piece
        total += contract(stack_ref[:, span], high, ((1,), (0,)))
        extra += contract(stack_ref[:rank, span], low, ((1,), (0,)))
    part_ref[0] = total[:rank] + total[rank:] + extra


def image_part(order, estimate, dual_var, covariance, basis, pieces, piece_width, first):
    rows = estimate.shape[0]
    rank = basis.shape[1] if first else basis.shape[0] // 2
    width = 256 if piece_width % 256 == 0 else 128
    per_piece = piece_width // width
    tile = pl.BlockSpec(
        (rows, width), lambda j, o: (0, o[j // per_piece] * per_piece + j % per_piece)
    )
    whole = pieces * piece_width
    vmem = pl.BlockSpec(memory_space=pltpu.VMEM)
    kept = pltpu.VMEM((rows, whole), jnp.bfloat16)
    stack = [jax.ShapeDtypeStruct((2 * rank, rows), jnp.bfloat16)] * first
    return pl.pallas_call(
        image_kernel,
        out_shape=(
            jax.ShapeDtypeStruct((pieces, rank, piece_width), jnp.float32), kept, kept, *stack
        ),
        grid_spec=pltpu.PrefetchScalarGridSpec(
            num_scalar_prefetch=1,
            grid=(pieces * per_piece,),
            in_specs=[tile, tile, tile, vmem],
            out_specs=[
                pl.BlockSpec((1, rank, width), lambda j, o: (j // per_piece, 0, j % per_piece)),
                vmem,
                vmem,
            ]
            + [vmem] * first,
        ),
        compiler_params=pltpu.CompilerParams(vmem_limit_bytes=14 * 2**20),
        name="image_part",
    )(order, in_hbm(estimate), in_hbm(dual_var), in_hbm(covariance), basis)


def product_kernel(*refs, counts, places, seeded):
    high_refs, refs = refs[: len(counts)], refs[len(counts) :]
    *piece_refs, out_ref, stack_ref = refs
    rows, rank = out_ref.shape
    if seeded:
        *piece_refs, prior_ref = piece_refs
    width = piece_refs[0].shape[1]
    for index, piece_ref in enumerate(piece_refs):
        high, low = split_two(piece_ref[...])
        stack_ref[:rank, index * width : (index + 1) * width] = high
        stack_ref[rank:, index * width : (index + 1) * width] = low
    depth = min(rows, 256)
    for start in range(0, rows, depth):
        span = slice(start, start + depth)
        both = jnp.zeros((depth, 2 * rank), jnp.float32)
        done = 0
        for high_ref, count, place in zip(high_refs, counts, places):
            there = slice(place * width, (place + count) * width)
            here = slice(done * width, (done + count) * width)
            both += contract(high_ref[span, there], stack_ref[:, here], ((1,), (1,)))
            done += count
        total = both[:, :rank] + both[:, rank:]
        out_ref[span, :] = prior_ref[span, :] + total if seeded else total


def product_part(highs, counts, places, pieces, prior=None):
    rows = highs[0].shape[0]
    rank, width = pieces[0].shape
    seeded = prior is not None
    vmem = pl.BlockSpec(memory_space=pltpu.VMEM)
    return pl.pallas_call(
        functools.partial(product_kernel, counts=counts, places=places, seeded=seeded),
        out_shape=jax.ShapeDtypeStruct((rows, rank), jnp.float32),
        in_specs=[vmem] * (len(highs) + len(pieces) + seeded),
        out_specs=vmem,
        scratch_shapes=[pltpu.VMEM((2 * rank, width * len(pieces)), jnp.bfloat16)],
        compiler_params=pltpu.CompilerParams(vmem_limit_bytes=12 * 2**20),
        name="product_part",
    )(*[in_vmem(high) for high in highs], *pieces, *([prior] * seeded))


def dot_three(left_side, right_side, dims=((1,), (0,))):
    left_high, left_low = split_two(left_side)
    right_high, right_low = split_two(right_side)
    return (
        contract(left_high, right_high, dims)
        + contract(left_low, right_high, dims)
        + contract(left_high, right_low, dims)
    )


def quadratic_kernel(where_ref, *refs):
    *piece_refs, product_ref, out_ref, small_ref, gram_ref = refs
    rank, width = piece_refs[0].shape
    small = jnp.zeros((rank, rank), jnp.float32)
    gram = jnp.zeros((rank, rank), jnp.float32)
    for index, piece_ref in enumerate(piece_refs):
        start = pl.multiple_of(where_ref[index] * width, width)
        small += dot_three(piece_ref[...], product_ref[pl.ds(start, width), :])
        gram += dot_three(piece_ref[...], piece_ref[...], ((1,), (1,)))
    small_ref[...] = small
    gram_ref[...] = gram
    lanes, _, share, _ = out_ref.shape
    for step in range(lanes):
        start = pl.multiple_of((where_ref[len(piece_refs)] ^ step) * share, share)
        out_ref[step, 0] = small_ref[pl.ds(start, share), :]
        out_ref[step, 1] = gram_ref[pl.ds(start, share), :]


def quadratic(order, pieces, product, lanes):
    rank = product.shape[1]
    vmem = pl.BlockSpec(memory_space=pltpu.VMEM)
    return pl.pallas_call(
        quadratic_kernel,
        out_shape=jax.ShapeDtypeStruct((lanes, 2, rank // lanes, rank), jnp.float32),
        in_specs=[pl.BlockSpec(memory_space=pltpu.SMEM)] + [vmem] * (len(pieces) + 1),
        out_specs=vmem,
        scratch_shapes=[pltpu.VMEM((rank, rank), jnp.float32)] * 2,
        compiler_params=pltpu.CompilerParams(vmem_limit_bytes=8 * 2**20),
        name="quadratic",
    )(order, *pieces, product)


def joined(where_ref, share_refs, whole_ref):
    share = share_refs[0].shape[0]
    lane = where_ref[where_ref.shape[0] - 1]
    for step, share_ref in enumerate(share_refs):
        start = pl.multiple_of((lane ^ step) * share, share)
        whole_ref[pl.ds(start, share), :] = share_ref[...]


def spread_row(band, index):
    return jnp.broadcast_to(band[index : index + 1, :], band.shape)


def spread_column(band, index):
    return jnp.broadcast_to(band[:, index : index + 1], band.shape)


def factor_kernel(where_ref, *refs):
    *share_refs, out_ref, gram_ref = refs
    joined(where_ref, share_refs, gram_ref)
    rank = gram_ref.shape[0]
    look = 4
    bands = rank // 8
    sublanes = lax.broadcasted_iota(jnp.int32, (8, rank), 0)
    lanes = lax.broadcasted_iota(jnp.int32, (8, rank), 1)
    left = [gram_ref[8 * i : 8 * i + 8, :] for i in range(bands)]
    right = [jnp.where(lanes == sublanes + 8 * i, 1.0, 0.0).astype(jnp.float32) for i in range(bands)]
    for start in range(0, rank, look):
        band, offset = start // 8, start % 8
        rows = [spread_row(left[band], offset + t) for t in range(look)]
        others = [spread_row(right[band], offset + t) for t in range(look)]
        small = [[spread_column(rows[t], start + u) for u in range(t + 1)] for t in range(look)]
        ratio = [[None] * look for _ in range(look)]
        scale = [None] * look
        for t in range(look):
            scale[t] = 1.0 / small[t][t]
            for v in range(t + 1, look):
                ratio[v][t] = small[v][t] * scale[t]
                for w in range(t + 1, v + 1):
                    small[v][w] = small[v][w] - ratio[v][t] * small[w][t]
                rows[v] = rows[v] - ratio[v][t] * rows[t]
                others[v] = others[v] - ratio[v][t] * others[t]
        for i in range(band, bands):
            columns = []
            for t in range(look):
                column = spread_column(left[i], start + t)
                for u in range(t):
                    column = column - ratio[t][u] * columns[u]
                columns.append(column)
            update, other = left[i], right[i]
            for t in range(look):
                amount = columns[t] * scale[t]
                update = update - amount * rows[t]
                other = other - amount * others[t]
            if i == band:
                final, final_other = left[i], right[i]
                for t in range(look):
                    root = lax.rsqrt(small[t][t])
                    final_other = jnp.where(sublanes == offset + t, others[t] * root, final_other)
                other = jnp.where(sublanes >= offset + look, other, final_other)
                update = jnp.where(sublanes >= offset + look, update, final)
            left[i], right[i] = update, other
    for i in range(bands):
        out_ref[8 * i : 8 * i + 8, :] = right[i]


def factor_of(order, shares):
    rank = shares[0].shape[1]
    vmem = pl.BlockSpec(memory_space=pltpu.VMEM)
    return pl.pallas_call(
        factor_kernel,
        out_shape=jax.ShapeDtypeStruct((rank, rank), jnp.float32),
        in_specs=[pl.BlockSpec(memory_space=pltpu.SMEM)] + [vmem] * len(shares),
        out_specs=vmem,
        scratch_shapes=[pltpu.VMEM((rank, rank), jnp.float32)],
        compiler_params=pltpu.CompilerParams(vmem_limit_bytes=4 * 2**20),
        name="factor",
    )(order, *shares)


def core_kernel(where_ref, inverse_ref, *refs):
    *share_refs, out_ref, small_ref = refs
    joined(where_ref, share_refs, small_ref)
    rank = small_ref.shape[0]
    row_ids = lax.broadcasted_iota(jnp.int32, (rank, rank), 0)
    col_ids = lax.broadcasted_iota(jnp.int32, (rank, rank), 1)
    identity = jnp.where(row_ids == col_ids, 1.0, 0.0).astype(jnp.float32)
    inverse = inverse_ref[...]
    raw = dot_three(dot_three(inverse, small_ref[...]), inverse, ((1,), (1,)))
    ritz = 0.5 * (raw + raw.T)
    square = dot_three(ritz, ritz) + 4.0 * penalty * identity
    frobenius = jnp.sqrt(jnp.sum(jnp.sum(square * square, axis=1, keepdims=True), axis=0, keepdims=True))

    def product(left_high, left_low, right_high, right_low):
        wide = jnp.concatenate([left_high, left_low], axis=1)
        twice = jnp.concatenate([right_high, right_high], axis=0)
        flat = ((1,), (0,))
        return contract(wide, twice, flat) + contract(left_high, right_low, flat)

    def newton(_, pair):
        high, low = split_two(pair)
        inner = product(high[rank:], low[rank:], high[:rank], low[:rank])
        factor = 0.5 * (3.0 * identity - inner)
        return product(high, low, *split_two(factor))

    pair = jnp.concatenate([square / frobenius, identity], axis=0)
    iterate = lax.fori_loop(0, NS_ITERS, newton, pair)[:rank]
    root = jnp.sqrt(frobenius) * iterate
    response = (ritz + root) / (2.0 * penalty) - base_level * identity
    out_ref[...] = dot_three(dot_three(inverse, response, ((0,), (0,))), inverse)


def core_of(order, inverse, shares):
    vmem = pl.BlockSpec(memory_space=pltpu.VMEM)
    return pl.pallas_call(
        core_kernel,
        out_shape=jax.ShapeDtypeStruct(inverse.shape, jnp.float32),
        in_specs=[pl.BlockSpec(memory_space=pltpu.SMEM)] + [vmem] * (1 + len(shares)),
        out_specs=vmem,
        scratch_shapes=[pltpu.VMEM(inverse.shape, jnp.float32)],
        compiler_params=pltpu.CompilerParams(vmem_limit_bytes=8 * 2**20),
        name="core",
    )(order, inverse, *shares)


def finish_kernel(place_ref, left_ref, core_ref, right_ref, *refs, groups, pieces, counts):
    *held_refs, est_ref, dual_ref, left_stack, right_twice, right_low = refs
    group = pl.program_id(0)
    piece = pl.program_id(1)
    height, width = est_ref.shape
    rank = core_ref.shape[0]

    @pl.when(group == 0)
    def _():
        weighted = dot_three(left_ref[0], core_ref[...], ((0,), (0,)))
        high, low = split_two(weighted)
        left_stack[piece, :, :rank] = high
        left_stack[piece, :, rank:] = low

    @pl.when(piece == 0)
    def _():
        high, low = split_two(right_ref[0])
        right_twice[:rank, :] = high
        right_twice[rank:, :] = high
        right_low[...] = low

    rows = pl.ds(pl.multiple_of(place_ref[groups + piece] * height, height), height)
    first, held = 0, None
    for held_ref, count in zip(held_refs, counts):
        at = jnp.clip(group - first, 0, count - 1)
        block = held_ref[rows, pl.ds(pl.multiple_of(at * width, width), width)]
        held = block if held is None else jnp.where(group >= first, block, held)
        first += count
    theta = contract(left_stack[piece], right_twice[...], ((1,), (0,)))
    theta += contract(left_stack[piece, :, :rank], right_low[...], ((1,), (0,)))
    row_ids = place_ref[groups + 2 * pieces] + place_ref[groups + piece] * height
    col_ids = place_ref[groups + 2 * pieces + 1] + place_ref[group] * width
    row_ids = row_ids + lax.broadcasted_iota(jnp.int32, (height, 1), 0)
    col_ids = col_ids + lax.broadcasted_iota(jnp.int32, (1, width), 1)
    theta = theta + jnp.where(row_ids == col_ids, base_level, 0.0)
    mixture = theta + held.astype(jnp.float32)
    clipped = jnp.clip(mixture, -threshold, threshold)
    est_ref[...] = mixture - clipped
    dual_ref[...] = clipped.astype(jnp.bfloat16)


def finish(place, left, core, right, held):
    pieces, rank, width = left.shape
    groups = right.shape[0]
    rows = pieces * width
    columns = groups * width
    vmem = pl.BlockSpec(memory_space=pltpu.VMEM)
    tile = pl.BlockSpec((width, width), lambda g, a, p: (p[groups + a], p[g]))
    return pl.pallas_call(
        functools.partial(
            finish_kernel, groups=groups, pieces=pieces, counts=[h.shape[1] // width for h in held]
        ),
        out_shape=(
            jax.ShapeDtypeStruct((rows, columns), jnp.float32),
            jax.ShapeDtypeStruct((rows, columns), jnp.bfloat16),
        ),
        grid_spec=pltpu.PrefetchScalarGridSpec(
            num_scalar_prefetch=1,
            grid=(groups, pieces),
            in_specs=[
                pl.BlockSpec((1, rank, width), lambda g, a, p: (jnp.where(g == 0, a, 0), 0, 0)),
                vmem,
                pl.BlockSpec((1, rank, width), lambda g, a, p: (g, 0, 0)),
            ]
            + [vmem] * len(held),
            out_specs=[tile, tile],
            scratch_shapes=[
                pltpu.VMEM((pieces, width, 2 * rank), jnp.bfloat16),
                pltpu.VMEM((2 * rank, width), jnp.bfloat16),
                pltpu.VMEM((rank, width), jnp.bfloat16),
            ],
        ),
        compiler_params=pltpu.CompilerParams(vmem_limit_bytes=14 * 2**20),
        name="finish",
    )(place, left, core, right, *[in_vmem(part) for part in held])


def blocked_body(*arguments):
    return blocked_steps(*arguments)


def blocked_steps(covariance, estimate, dual_var, start_basis):
    n_row, n_col = lax.axis_size("row"), lax.axis_size("col")
    lanes = n_row // n_col
    row_index, col_index = lax.axis_index("row"), lax.axis_index("col")
    lane, chip = row_index % lanes, row_index // lanes
    rows, columns = estimate.shape
    width = columns // n_row

    def across_lanes(value, step):
        route = [(r, r // lanes * lanes + (r % lanes ^ step)) for r in range(n_row)]
        return lax.ppermute(value, "row", route)

    def across_chips(value, step):
        route = [(r, (r // lanes ^ step) * lanes + r % lanes) for r in range(n_row)]
        return lax.ppermute(value, "row", route)

    def across_columns(value, step):
        return lax.ppermute(value, "col", [(c, c ^ step) for c in range(n_col)])

    def total_of(value, move, count):
        arrived = []
        for step in range(1, count):
            arrived.append(move(value, step))
        return sum(arrived, value)

    def block_at(step, s):
        return (lane ^ step) * n_col + (chip ^ s)

    calls = [[(step, s) for s in range(1, n_col)] for step in reversed(range(lanes))]
    calls.append([(step, 0) for step in reversed(range(lanes))])
    orders = [jnp.stack([block_at(*at) for at in call]).astype(jnp.int32) for call in calls]
    piece_rows = jnp.stack([col_index ^ a for a in range(n_col)]).astype(jnp.int32)
    corner = jnp.stack([row_index * rows, col_index * columns]).astype(jnp.int32)
    place = jnp.concatenate(orders + [piece_rows, piece_rows, corner])
    piece_rows = jnp.concatenate([piece_rows, lane.reshape(1).astype(jnp.int32)])
    local = jnp.broadcast_to(chip == col_index, (8, 128)).astype(jnp.float32)
    orders, piece_rows, place, local = lax.optimization_barrier((orders, piece_rows, place, local))

    part, high, held, basis = {}, [], [], in_hbm(start_basis)
    for index, call in enumerate(calls):
        if index == lanes:
            gathered = sum([part[step] for step in range(1, lanes)], part[0])
            gathered, orders[index] = lax.optimization_barrier((gathered, orders[index]))
        out = image_part(
            orders[index], estimate, dual_var, covariance, basis, len(call), width, index == 0
        )
        if index == 0:
            basis = out[3]
        high.append(out[1])
        held.append(out[2])
        step = call[0][0]
        if index < lanes:
            if step:
                part[step] = across_lanes(out[0], step)
            else:
                part[0] = out[0]
    last = out[0]
    own = last[lanes - 1]
    for index in range(lanes - 1):
        own = own + across_lanes(last[index], calls[-1][index][0])
    for s in range(1, n_col):
        arrived = across_chips(gathered[s - 1], s)
        own = own + arrived
    half = [own]
    for s in range(1, n_col):
        half.append(across_chips(own, s))
    arrivals = []
    for a in range(n_col):
        route = [
            (r * n_col + c, (c * lanes + r % lanes) * n_col + (r // lanes ^ a))
            for r in range(n_row)
            for c in range(n_col)
            if r // lanes ^ a != c
        ]
        arrivals.append(lax.ppermute(own, ("row", "col"), route))
    right = {(0, s): half[s] for s in range(n_col)}
    for step in range(1, lanes):
        for s in range(n_col):
            right[step, s] = across_lanes(half[s], step)
    product = None
    for step in range(lanes):
        at = lanes - 1 - step
        product = product_part(
            [high[at], high[lanes]],
            (n_col - 1, 1),
            (0, at),
            [right[step, s] for s in range(1, n_col)] + [right[step, 0]],
            product,
        )
    local, product = lax.optimization_barrier((local, product))
    left = [jnp.where(local[:1, :1] > 0.5, half[a], arrivals[a]) for a in range(n_col)]
    shares = quadratic(piece_rows, left, product, lanes)
    both = sum([across_lanes(shares[step], step) for step in range(1, lanes)], shares[0])
    both = total_of(both, across_chips, n_col)
    small, gram = lax.optimization_barrier((both[0], both[1]))

    def of_lanes(share):
        return [share] + [across_lanes(share, step) for step in range(1, lanes)]

    grams = of_lanes(gram)
    inverse = factor_of(piece_rows, grams)
    small = total_of(small, across_columns, n_col)
    smalls = of_lanes(small)
    core = core_of(piece_rows, inverse, smalls)
    right_all = jnp.stack([right[at] for call in calls for at in call])
    return finish(place, jnp.stack(left), core, right_all, held)


def power_of_two(count):
    return count & (count - 1) == 0


def chosen_body(mesh):
    n_row, n_col = mesh.shape["row"], mesh.shape["col"]

    def pick(covariance, estimate, dual_var, start_basis):
        rows, columns = estimate.shape
        fits = n_row % n_col == 0 and power_of_two(n_row) and power_of_two(n_col)
        fits = fits and columns % (128 * n_row) == 0 and rows * n_row == columns * n_col
        fits = fits and start_basis.shape[1] % 128 == 0
        chosen = blocked_body if fits else body
        return chosen(covariance, estimate, dual_var, start_basis)

    return pick


def solution(mesh):
    return jax.shard_map(
        chosen_body(mesh),
        mesh=mesh,
        in_specs=(P("row", "col"), P("row", "col"), P("row", "col"), P("row", None)),
        out_specs=(P("row", "col"), P("row", "col")),
        check_vma=False,
    )
```

profile of v0, /device:TPU:0, one launch (start us, length us, event | category | flops | bytes accessed | tf_op | source)
XLA Modules:
  0.0 149.8 jit_solution(7294732078987719575)
XLA Ops:
  1.0 11.7 %image_part.3 = (f32[3,128,512]{2,1,0:T(8,128)S(1)}, bf16[2048,1536]{1,0:T(8,128)(2,1)S(1)}, bf16[2048,1536]{1,0:T(8,128)(2,1)S(1)}, bf16[256,2048]{1,0:T(8,128)(2,1)S(1)}) custom-call(s32[3]{0:T(128)S(1)} %get-tuple-element.26.order_ref, bf16[2048,4096]{1,0:T(8,128)(2,1)} %est_ref.5, bf16[2048,4096]{1,0:T(8,128)(2,1)} %dual_ref.5, ...), custom_call_target="tpu_custom_call" | custom-call | tf_op jit(solution)/shard_map/image_part/pallas_call | solution.py:187
  12.7 0.6 collective-permute-start
  13.3 10.7 %image_part.4 = (f32[3,128,512]{2,1,0:T(8,128)S(1)}, bf16[2048,1536]{1,0:T(8,128)(2,1)S(1)}, bf16[2048,1536]{1,0:T(8,128)(2,1)S(1)}) custom-call(s32[3]{0:T(128)S(1)} %get-tuple-element.28.order_ref, bf16[2048,4096]{1,0:T(8,128)(2,1)} %est_ref.5, bf16[2048,4096]{1,0:T(8,128)(2,1)} %dual_ref.5, bf16[2048,4096]{1,0:T(8,128)(2,1)} %cov_ref.5, ...), custom_call_target="tpu_custom_call" | custom-call | tf_op jit(solution)/shard_map/image_part/pallas_call | solution.py:187
  24.2 2.5 %collective-permute-start.2 = (f32[128,512]{1,0:T(8,128)S(1)}, f32[128,512]{1,0:T(8,128)S(1)}, u32[]{:S(2)}, u32[]{:S(2)}) collective-permute-start(f32[128,512]{1,0:T(8,128)S(1)} %get-tuple-element.46), channel_id=1, source_target_pairs={{0,8},{4,12},{8,0},{12,4},{16,24},{20,28},{24,16},{28,20},{1,9},{5... | collective-permute-start | bytes 786440 | tf_op jit(solution)/shard_map/ppermute | solution.py:510
  26.7 1.5 collective-permute-start.4
  28.3 7.6 %image_part.5 = (f32[2,128,512]{2,1,0:T(8,128)S(1)}, bf16[2048,1024]{1,0:T(8,128)(2,1)S(1)}, bf16[2048,1024]{1,0:T(8,128)(2,1)S(1)}) custom-call(s32[2]{0:T(128)S(1)} %pad_add_fusion.2.order_ref, bf16[2048,4096]{1,0:T(8,128)(2,1)} %est_ref.5, bf16[2048,4096]{1,0:T(8,128)(2,1)} %dual_ref.5, bf16[2048,4096]{1,0:T(8,128)(2,1)} %cov_ref.5, ...), custom_call_target="tpu_custom_call" | custom-call | tf_op jit(solution)/shard_map/image_part/pallas_call | solution.py:187
  36.0 4.6 %collective-permute-done.4 = f32[128,512]{1,0:T(8,128)S(1)} collective-permute-done((f32[128,512]{1,0:T(8,128)S(1)}, f32[128,512]{1,0:T(8,128)S(1)}, u32[]{:S(2)}, u32[]{:S(2)}) %collective-permute-start.4) | collective-permute-done | bytes 262176 | tf_op jit(solution)/shard_map/ppermute | solution.py:510
  40.6 1.4 collective-permute-done.3
  42.1 1.5 %collective-permute-start.9 = (f32[128,512]{1,0:T(8,128)S(1)}, f32[128,512]{1,0:T(8,128)S(1)}, u32[]{:S(2)}, u32[]{:S(2)}) collective-permute-start(f32[128,512]{1,0:T(8,128)S(1)} %fusion.2.refs_5_), channel_id=1, source_target_pairs={{0,24},{4,28},{8,16},{12,20},{16,8},{20,12},{24,0},{28,4},{1,25},{... | collective-permute-start | bytes 786440 | tf_op jit(solution)/shard_map/ppermute | solution.py:510
  43.6 1.5 %collective-permute-start.7 = (f32[128,512]{1,0:T(8,128)S(1)}, f32[128,512]{1,0:T(8,128)S(1)}, u32[]{:S(2)}, u32[]{:S(2)}) collective-permute-start(f32[128,512]{1,0:T(8,128)S(1)} %fusion.2.refs_5_), channel_id=1, source_target_pairs={{0,16},{4,20},{8,24},{12,28},{16,0},{20,4},{24,8},{28,12},{1,17},{... | collective-permute-start | bytes 786440 | tf_op jit(solution)/shard_map/ppermute | solution.py:510
  45.7 6.6 %collective-permute-done.9.refs_4_ = f32[128,512]{1,0:T(8,128)S(1)} collective-permute-done((f32[128,512]{1,0:T(8,128)S(1)}, f32[128,512]{1,0:T(8,128)S(1)}, u32[]{:S(2)}, u32[]{:S(2)}) %collective-permute-start.9) | collective-permute-done | bytes 262176 | tf_op jit(solution)/shard_map/ppermute | solution.py:510
  52.3 3.7 %collective-permute-done.7.refs_3_ = f32[128,512]{1,0:T(8,128)S(1)} collective-permute-done((f32[128,512]{1,0:T(8,128)S(1)}, f32[128,512]{1,0:T(8,128)S(1)}, u32[]{:S(2)}, u32[]{:S(2)}) %collective-permute-start.7) | collective-permute-done | bytes 262176 | tf_op jit(solution)/shard_map/ppermute | solution.py:510
  56.5 3.5 %collective-permute-start.13 = (f32[128,512]{1,0:T(8,128)S(1)}, f32[128,512]{1,0:T(8,128)S(1)}, u32[]{:S(2)}, u32[]{:S(2)}) collective-permute-start(f32[128,512]{1,0:T(8,128)S(1)} %fusion.2.refs_5_), channel_id=1, source_target_pairs={{0,1},{2,17},{3,25},{4,5},{6,21},{7,29},{9,8},{10,16},{11,24},{13,... | collective-permute-start | bytes 786440 | tf_op jit(solution)/shard_map/ppermute | solution.py:570
  60.0 3.3 %collective-permute-start.14 = (f32[128,512]{1,0:T(8,128)S(1)}, f32[128,512]{1,0:T(8,128)S(1)}, u32[]{:S(2)}, u32[]{:S(2)}) collective-permute-start(f32[128,512]{1,0:T(8,128)S(1)} %fusion.2.refs_5_), channel_id=1, source_target_pairs={{0,2},{1,10},{3,26},{4,6},{5,14},{7,30},{8,3},{9,11},{10,19},{12,7... | collective-permute-start | bytes 786440 | tf_op jit(solution)/shard_map/ppermute | solution.py:570
  63.3 2.4 %product_part.2.refs_6_ = f32[2048,128]{1,0:T(8,128)S(1)} custom-call(bf16[2048,1536]{1,0:T(8,128)(2,1)S(1)} %get-tuple-element.37.refs_0_, bf16[2048,1024]{1,0:T(8,128)(2,1)S(1)} %get-tuple-element.34.refs_1_, f32[128,512]{1,0:T(8,128)S(1)} %collective-permute-done.5.refs_2_, f32[128,512]{1,0:T(8,128)S(1)} %collective-permute-done.7.refs_3_, ...), custom_call_target="tpu_custom_call" | custom-call | tf_op jit(solution)/shard_map/product_part/pallas_call | solution.py:238
  65.7 3.8 %collective-permute-start.15 = (f32[128,512]{1,0:T(8,128)S(1)}, f32[128,512]{1,0:T(8,128)S(1)}, u32[]{:S(2)}, u32[]{:S(2)}) collective-permute-start(f32[128,512]{1,0:T(8,128)S(1)} %fusion.2.refs_5_), channel_id=1, source_target_pairs={{0,3},{1,11},{2,19},{4,7},{5,15},{6,23},{8,2},{9,10},{11,26},{12,6... | collective-permute-start | bytes 786440 | tf_op jit(solution)/shard_map/ppermute | solution.py:570
  69.5 0.9 collective-permute-start.12
  70.3 2.4 %product_part.3.refs_4_ = f32[2048,128]{1,0:T(8,128)S(1)} custom-call(bf16[2048,1536]{1,0:T(8,128)(2,1)S(1)} %get-tuple-element.27.refs_0_, bf16[2048,1024]{1,0:T(8,128)(2,1)S(1)} %get-tuple-element.34.refs_1_, f32[128,512]{1,0:T(8,128)S(1)} %collective-permute-done.6.refs_2_, f32[128,512]{1,0:T(8,128)S(1)} %collective-permute-done.8.refs_3_, ...), custom_call_target="tpu_custom_call" | custom-call | tf_op jit(solution)/shard_map/product_part/pallas_call | solution.py:238
  74.0 3.0 %collective-permute-done.15 = f32[128,512]{1,0:T(8,128)S(1)} collective-permute-done((f32[128,512]{1,0:T(8,128)S(1)}, f32[128,512]{1,0:T(8,128)S(1)}, u32[]{:S(2)}, u32[]{:S(2)}) %collective-permute-start.15) | collective-permute-done | bytes 262176 | tf_op jit(solution)/shard_map/ppermute | solution.py:570
  77.1 1.5 %quadratic.1 = f32[2,2,64,128]{3,2,1,0:T(8,128)S(1)} custom-call(s32[5]{0:T(128)S(1)} %concatenate.8.where_ref, f32[128,512]{1,0:T(8,128)S(1)} %broadcast_select_fusion.3.refs_0_, f32[128,512]{1,0:T(8,128)S(1)} %broadcast_select_fusion.2.refs_1_, f32[128,512]{1,0:T(8,128)S(1)} %broadcast_select_fusion.1.refs_2_, ...), custom_call_target="tpu_custom_call" | custom-call | tf_op jit(solution)/shard_map/quadratic/pallas_call | solution.py:280
  78.9 1.1 collective-permute-done.16
  80.0 6.3 %collective-permute-start.19 = (f32[2,64,128]{2,1,0:T(8,128)S(1)}, f32[2,64,128]{2,1,0:T(8,128)S(1)}, u32[]{:S(2)}, u32[]{:S(2)}) collective-permute-start(f32[2,64,128]{2,1,0:T(8,128)S(1)} %fusion.3), channel_id=1, source_target_pairs={{0,24},{4,28},{8,16},{12,20},{16,8},{20,12},{24,0},{28,4},{1,25},{... | collective-permute-start | bytes 196616 | tf_op jit(solution)/shard_map/ppermute | solution.py:510
  86.3 10.9 %collective-permute-start.18 = (f32[2,64,128]{2,1,0:T(8,128)S(1)}, f32[2,64,128]{2,1,0:T(8,128)S(1)}, u32[]{:S(2)}, u32[]{:S(2)}) collective-permute-start(f32[2,64,128]{2,1,0:T(8,128)S(1)} %fusion.3), channel_id=1, source_target_pairs={{0,16},{4,20},{8,24},{12,28},{16,0},{20,4},{24,8},{28,12},{1,17},{... | collective-permute-start | bytes 196616 | tf_op jit(solution)/shard_map/ppermute | solution.py:510
  97.3 2.2 %collective-permute-done.18 = f32[2,64,128]{2,1,0:T(8,128)S(1)} collective-permute-done((f32[2,64,128]{2,1,0:T(8,128)S(1)}, f32[2,64,128]{2,1,0:T(8,128)S(1)}, u32[]{:S(2)}, u32[]{:S(2)}) %collective-permute-start.18) | collective-permute-done | bytes 65568 | tf_op jit(solution)/shard_map/ppermute | solution.py:510
  99.5 2.0 %collective-permute-done.17 = f32[2,64,128]{2,1,0:T(8,128)S(1)} collective-permute-done((f32[2,64,128]{2,1,0:T(8,128)S(1)}, f32[2,64,128]{2,1,0:T(8,128)S(1)}, u32[]{:S(2)}, u32[]{:S(2)}) %collective-permute-start.17) | collective-permute-done | bytes 65568 | tf_op jit(solution)/shard_map/ppermute | solution.py:510
  101.5 1.8 %collective-permute-start.23 = (f32[64,128]{1,0:T(8,128)S(1)}, f32[64,128]{1,0:T(8,128)S(1)}, u32[]{:S(2)}, u32[]{:S(2)}) collective-permute-start(f32[64,128]{1,0:T(8,128)S(1)} %get-tuple-element.42), channel_id=1, source_target_pairs={{0,3},{1,2},{2,1},{3,0},{4,7},{5,6},{6,5},{7,4},{8,11},{9,10},{10,... | collective-permute-start | bytes 98312 | tf_op jit(solution)/shard_map/ppermute | solution.py:513
  103.3 2.7 %collective-permute-start.21 = (f32[64,128]{1,0:T(8,128)S(1)}, f32[64,128]{1,0:T(8,128)S(1)}, u32[]{:S(2)}, u32[]{:S(2)}) collective-permute-start(f32[64,128]{1,0:T(8,128)S(1)} %get-tuple-element.42), channel_id=1, source_target_pairs={{0,1},{1,0},{2,3},{3,2},{4,5},{5,4},{6,7},{7,6},{8,9},{9,8},{10,11... | collective-permute-start | bytes 98312 | tf_op jit(solution)/shard_map/ppermute | solution.py:513
  106.1 1.3 collective-permute-done.23
  107.4 0.8 collective-permute-done.22
  108.4 6.4 %factor.1.inverse_ref = f32[128,128]{1,0:T(8,128)S(1)} custom-call(s32[5]{0:T(128)S(1)} %concatenate.8.where_ref, f32[64,128]{1,0:T(8,128)S(1)} %get-tuple-element.41.refs_0_, f32[64,128]{1,0:T(8,128)S(1)} %collective-permute-done.20.refs_1_), custom_call_target="tpu_custom_call" | custom-call | tf_op jit(solution)/shard_map/factor/pallas_call | solution.py:359
  114.8 6.2 %core.1.core_ref = f32[128,128]{1,0:T(8,128)S(1)} custom-call(s32[5]{0:T(128)S(1)} %concatenate.8.where_ref, f32[128,128]{1,0:T(8,128)S(1)} %factor.1.inverse_ref, f32[64,128]{1,0:T(8,128)S(1)} %add_add_fusion.1.refs_0_, f32[64,128]{1,0:T(8,128)S(1)} %collective-permute-done.24.refs_1_), custom_call_target="tpu_custom_call" | custom-call | tf_op jit(solution)/shard_map/core/pallas_call | solution.py:404
  121.0 28.7 %finish.1 = (f32[2048,4096]{1,0:T(8,128)}, bf16[2048,4096]{1,0:T(8,128)(2,1)}) custom-call(s32[18]{0:T(128)S(1)} %concatenate.9.place_ref, f32[4,128,512]{2,1,0:T(8,128)S(1)} %pad_maximum_fusion.left_ref, f32[128,128]{1,0:T(8,128)S(1)} %core.1.core_ref, f32[8,128,512]{2,1,0:T(8,128)S(1)} %bitcast_dynamic-update-slice_fusion.right_ref, ...), custom_call_target="tpu_custom_call" | custom-call | tf_op jit(solution)/shard_map/finish/pallas_call | solution.py:463
  (55 shorter events, 3.1 us)
Async XLA Ops:
  12.7 11.3 %collective-permute-start = (f32[3,128,512]{2,1,0:T(8,128)S(1)}, f32[3,128,512]{2,1,0:T(8,128)S(1)}, u32[]{:S(2)}, u32[]{:S(2)}) collective-permute-start(f32[3,128,512]{2,1,0:T(8,128)S(1)} %get-tuple-element.31), channel_id=1, source_target_pairs={{0,4},{4,0},{8,12},{12,8},{16,20},{20,16},{24,28},{28,24},{1,5},{5... | collective-permute-start | bytes 2359304 | tf_op jit(solution)/shard_map/ppermute | solution.py:506
  24.2 11.8 %collective-permute-start.2 = (f32[128,512]{1,0:T(8,128)S(1)}, f32[128,512]{1,0:T(8,128)S(1)}, u32[]{:S(2)}, u32[]{:S(2)}) collective-permute-start(f32[128,512]{1,0:T(8,128)S(1)} %get-tuple-element.46), channel_id=1, source_target_pairs={{0,8},{4,12},{8,0},{12,4},{16,24},{20,28},{24,16},{28,20},{1,9},{5... | collective-permute-start | bytes 786440 | tf_op jit(solution)/shard_map/ppermute | solution.py:510
  26.7 13.9 %collective-permute-start.4 = (f32[128,512]{1,0:T(8,128)S(1)}, f32[128,512]{1,0:T(8,128)S(1)}, u32[]{:S(2)}, u32[]{:S(2)}) collective-permute-start(f32[128,512]{1,0:T(8,128)S(1)} %get-tuple-element.47), channel_id=1, source_target_pairs={{0,24},{4,28},{8,16},{12,20},{16,8},{20,12},{24,0},{28,4},{1,25},{... | collective-permute-start | bytes 786440 | tf_op jit(solution)/shard_map/ppermute | solution.py:510
  28.2 13.8 %collective-permute-start.3 = (f32[128,512]{1,0:T(8,128)S(1)}, f32[128,512]{1,0:T(8,128)S(1)}, u32[]{:S(2)}, u32[]{:S(2)}) collective-permute-start(f32[128,512]{1,0:T(8,128)S(1)} %get-tuple-element.48), channel_id=1, source_target_pairs={{0,16},{4,20},{8,24},{12,28},{16,0},{20,4},{24,8},{28,12},{1,17},{... | collective-permute-start | bytes 786440 | tf_op jit(solution)/shard_map/ppermute | solution.py:510
  35.9 6.1 %collective-permute-start.1 = (f32[128,512]{1,0:T(8,128)S(1)}, f32[128,512]{1,0:T(8,128)S(1)}, u32[]{:S(2)}, u32[]{:S(2)}) collective-permute-start(f32[128,512]{1,0:T(8,128)S(1)} %slice_bitcast_fusion.3), channel_id=1, source_target_pairs={{0,4},{4,0},{8,12},{12,8},{16,20},{20,16},{24,28},{28,24},{1,5},{5... | collective-permute-start | bytes 786440 | tf_op jit(solution)/shard_map/ppermute | solution.py:506
  42.1 10.2 %collective-permute-start.9 = (f32[128,512]{1,0:T(8,128)S(1)}, f32[128,512]{1,0:T(8,128)S(1)}, u32[]{:S(2)}, u32[]{:S(2)}) collective-permute-start(f32[128,512]{1,0:T(8,128)S(1)} %fusion.2.refs_5_), channel_id=1, source_target_pairs={{0,24},{4,28},{8,16},{12,20},{16,8},{20,12},{24,0},{28,4},{1,25},{... | collective-permute-start | bytes 786440 | tf_op jit(solution)/shard_map/ppermute | solution.py:510
  43.6 12.4 %collective-permute-start.7 = (f32[128,512]{1,0:T(8,128)S(1)}, f32[128,512]{1,0:T(8,128)S(1)}, u32[]{:S(2)}, u32[]{:S(2)}) collective-permute-start(f32[128,512]{1,0:T(8,128)S(1)} %fusion.2.refs_5_), channel_id=1, source_target_pairs={{0,16},{4,20},{8,24},{12,28},{16,0},{20,4},{24,8},{28,12},{1,17},{... | collective-permute-start | bytes 786440 | tf_op jit(solution)/shard_map/ppermute | solution.py:510
  45.1 10.9 %collective-permute-start.5 = (f32[128,512]{1,0:T(8,128)S(1)}, f32[128,512]{1,0:T(8,128)S(1)}, u32[]{:S(2)}, u32[]{:S(2)}) collective-permute-start(f32[128,512]{1,0:T(8,128)S(1)} %fusion.2.refs_5_), channel_id=1, source_target_pairs={{0,8},{4,12},{8,0},{12,4},{16,24},{20,28},{24,16},{28,20},{1,9},{5... | collective-permute-start | bytes 786440 | tf_op jit(solution)/shard_map/ppermute | solution.py:510
  45.7 14.3 %collective-permute-start.11 = (f32[128,512]{1,0:T(8,128)S(1)}, f32[128,512]{1,0:T(8,128)S(1)}, u32[]{:S(2)}, u32[]{:S(2)}) collective-permute-start(f32[128,512]{1,0:T(8,128)S(1)} %fusion.2.refs_5_), channel_id=1, source_target_pairs={{0,4},{4,0},{8,12},{12,8},{16,20},{20,16},{24,28},{28,24},{1,5},{5... | collective-permute-start | bytes 786440 | tf_op jit(solution)/shard_map/ppermute | solution.py:506
  52.3 13.4 %collective-permute-start.10 = (f32[128,512]{1,0:T(8,128)S(1)}, f32[128,512]{1,0:T(8,128)S(1)}, u32[]{:S(2)}, u32[]{:S(2)}) collective-permute-start(f32[128,512]{1,0:T(8,128)S(1)} %collective-permute-done.9.refs_4_), channel_id=1, source_target_pairs={{0,4},{4,0},{8,12},{12,8},{16,20},{20,16},{24,28},{28,24},{1,5},{5... | collective-permute-start | bytes 786440 | tf_op jit(solution)/shard_map/ppermute | solution.py:506
  56.0 13.5 %collective-permute-start.8 = (f32[128,512]{1,0:T(8,128)S(1)}, f32[128,512]{1,0:T(8,128)S(1)}, u32[]{:S(2)}, u32[]{:S(2)}) collective-permute-start(f32[128,512]{1,0:T(8,128)S(1)} %collective-permute-done.7.refs_3_), channel_id=1, source_target_pairs={{0,4},{4,0},{8,12},{12,8},{16,20},{20,16},{24,28},{28,24},{1,5},{5... | collective-permute-start | bytes 786440 | tf_op jit(solution)/shard_map/ppermute | solution.py:506
  56.0 14.3 %collective-permute-start.6 = (f32[128,512]{1,0:T(8,128)S(1)}, f32[128,512]{1,0:T(8,128)S(1)}, u32[]{:S(2)}, u32[]{:S(2)}) collective-permute-start(f32[128,512]{1,0:T(8,128)S(1)} %collective-permute-done.5.refs_2_), channel_id=1, source_target_pairs={{0,4},{4,0},{8,12},{12,8},{16,20},{20,16},{24,28},{28,24},{1,5},{5... | collective-permute-start | bytes 786440 | tf_op jit(solution)/shard_map/ppermute | solution.py:506
  56.5 17.4 %collective-permute-start.13 = (f32[128,512]{1,0:T(8,128)S(1)}, f32[128,512]{1,0:T(8,128)S(1)}, u32[]{:S(2)}, u32[]{:S(2)}) collective-permute-start(f32[128,512]{1,0:T(8,128)S(1)} %fusion.2.refs_5_), channel_id=1, source_target_pairs={{0,1},{2,17},{3,25},{4,5},{6,21},{7,29},{9,8},{10,16},{11,24},{13,... | collective-permute-start | bytes 786440 | tf_op jit(solution)/shard_map/ppermute | solution.py:570
  60.0 14.0 %collective-permute-start.14 = (f32[128,512]{1,0:T(8,128)S(1)}, f32[128,512]{1,0:T(8,128)S(1)}, u32[]{:S(2)}, u32[]{:S(2)}) collective-permute-start(f32[128,512]{1,0:T(8,128)S(1)} %fusion.2.refs_5_), channel_id=1, source_target_pairs={{0,2},{1,10},{3,26},{4,6},{5,14},{7,30},{8,3},{9,11},{10,19},{12,7... | collective-permute-start | bytes 786440 | tf_op jit(solution)/shard_map/ppermute | solution.py:570
  65.7 11.3 %collective-permute-start.15 = (f32[128,512]{1,0:T(8,128)S(1)}, f32[128,512]{1,0:T(8,128)S(1)}, u32[]{:S(2)}, u32[]{:S(2)}) collective-permute-start(f32[128,512]{1,0:T(8,128)S(1)} %fusion.2.refs_5_), channel_id=1, source_target_pairs={{0,3},{1,11},{2,19},{4,7},{5,15},{6,23},{8,2},{9,10},{11,26},{12,6... | collective-permute-start | bytes 786440 | tf_op jit(solution)/shard_map/ppermute | solution.py:570
  69.5 7.6 %collective-permute-start.12 = (f32[128,512]{1,0:T(8,128)S(1)}, f32[128,512]{1,0:T(8,128)S(1)}, u32[]{:S(2)}, u32[]{:S(2)}) collective-permute-start(f32[128,512]{1,0:T(8,128)S(1)} %fusion.2.refs_5_), channel_id=1, source_target_pairs={{1,8},{2,16},{3,24},{5,12},{6,20},{7,28},{8,1},{10,17},{11,25},{12... | collective-permute-start | bytes 786440 | tf_op jit(solution)/shard_map/ppermute | solution.py:570
  78.7 1.3 collective-permute-start.16
  80.0 17.3 %collective-permute-start.19 = (f32[2,64,128]{2,1,0:T(8,128)S(1)}, f32[2,64,128]{2,1,0:T(8,128)S(1)}, u32[]{:S(2)}, u32[]{:S(2)}) collective-permute-start(f32[2,64,128]{2,1,0:T(8,128)S(1)} %fusion.3), channel_id=1, source_target_pairs={{0,24},{4,28},{8,16},{12,20},{16,8},{20,12},{24,0},{28,4},{1,25},{... | collective-permute-start | bytes 196616 | tf_op jit(solution)/shard_map/ppermute | solution.py:510
  86.3 13.2 %collective-permute-start.18 = (f32[2,64,128]{2,1,0:T(8,128)S(1)}, f32[2,64,128]{2,1,0:T(8,128)S(1)}, u32[]{:S(2)}, u32[]{:S(2)}) collective-permute-start(f32[2,64,128]{2,1,0:T(8,128)S(1)} %fusion.3), channel_id=1, source_target_pairs={{0,16},{4,20},{8,24},{12,28},{16,0},{20,4},{24,8},{28,12},{1,17},{... | collective-permute-start | bytes 196616 | tf_op jit(solution)/shard_map/ppermute | solution.py:510
  97.2 4.3 %collective-permute-start.17 = (f32[2,64,128]{2,1,0:T(8,128)S(1)}, f32[2,64,128]{2,1,0:T(8,128)S(1)}, u32[]{:S(2)}, u32[]{:S(2)}) collective-permute-start(f32[2,64,128]{2,1,0:T(8,128)S(1)} %fusion.3), channel_id=1, source_target_pairs={{0,8},{4,12},{8,0},{12,4},{16,24},{20,28},{24,16},{28,20},{1,9},{5... | collective-permute-start | bytes 196616 | tf_op jit(solution)/shard_map/ppermute | solution.py:510
  101.5 5.9 %collective-permute-start.23 = (f32[64,128]{1,0:T(8,128)S(1)}, f32[64,128]{1,0:T(8,128)S(1)}, u32[]{:S(2)}, u32[]{:S(2)}) collective-permute-start(f32[64,128]{1,0:T(8,128)S(1)} %get-tuple-element.42), channel_id=1, source_target_pairs={{0,3},{1,2},{2,1},{3,0},{4,7},{5,6},{6,5},{7,4},{8,11},{9,10},{10,... | collective-permute-start | bytes 98312 | tf_op jit(solution)/shard_map/ppermute | solution.py:513
  103.3 4.9 %collective-permute-start.22 = (f32[64,128]{1,0:T(8,128)S(1)}, f32[64,128]{1,0:T(8,128)S(1)}, u32[]{:S(2)}, u32[]{:S(2)}) collective-permute-start(f32[64,128]{1,0:T(8,128)S(1)} %get-tuple-element.42), channel_id=1, source_target_pairs={{0,2},{1,3},{2,0},{3,1},{4,6},{5,7},{6,4},{7,5},{8,10},{9,11},{10,... | collective-permute-start | bytes 98312 | tf_op jit(solution)/shard_map/ppermute | solution.py:513
  103.3 4.9 %collective-permute-start.21 = (f32[64,128]{1,0:T(8,128)S(1)}, f32[64,128]{1,0:T(8,128)S(1)}, u32[]{:S(2)}, u32[]{:S(2)}) collective-permute-start(f32[64,128]{1,0:T(8,128)S(1)} %get-tuple-element.42), channel_id=1, source_target_pairs={{0,1},{1,0},{2,3},{3,2},{4,5},{5,4},{6,7},{7,6},{8,9},{9,8},{10,11... | collective-permute-start | bytes 98312 | tf_op jit(solution)/shard_map/ppermute | solution.py:513
  106.0 2.4 %collective-permute-start.20 = (f32[64,128]{1,0:T(8,128)S(1)}, f32[64,128]{1,0:T(8,128)S(1)}, u32[]{:S(2)}, u32[]{:S(2)}) collective-permute-start(f32[64,128]{1,0:T(8,128)S(1)} %get-tuple-element.41.refs_0_), channel_id=1, source_target_pairs={{0,4},{4,0},{8,12},{12,8},{16,20},{20,16},{24,28},{28,24},{1,5},{5... | collective-permute-start | bytes 98312 | tf_op jit(solution)/shard_map/ppermute | solution.py:506
  108.2 6.6 %collective-permute-start.24 = (f32[64,128]{1,0:T(8,128)S(1)}, f32[64,128]{1,0:T(8,128)S(1)}, u32[]{:S(2)}, u32[]{:S(2)}) collective-permute-start(f32[64,128]{1,0:T(8,128)S(1)} %add_add_fusion.1.refs_0_), channel_id=1, source_target_pairs={{0,4},{4,0},{8,12},{12,8},{16,20},{20,16},{24,28},{28,24},{1,5},{5... | collective-permute-start | bytes 98312 | tf_op jit(solution)/shard_map/ppermute | solution.py:506
where the time goes:
time: 150 us
  Pallas kernels  77.6 us (52%)
  starting transfers between devices  42.1 us (28%)
  waiting for transfers between devices  26.7 us (18%)
  between operations  1.71 us (1%)
    pallas_call x3, Pallas kernels, image_part(): pl.pallas_call(image_kernel, out_shape=(jax.ShapeDtypeStruct((pieces, ran...  30 us
    pallas_call x1, Pallas kernels, finish(): pl.pallas_call(functools.partial(finish_kernel, groups=groups, pieces=pie...  28.7 us
    ppermute x9, starting transfers between devices, across_chips(): return lax.ppermute(value, 'row', route)  24.9 us
    ppermute x9, waiting for transfers between devices, across_chips(): return lax.ppermute(value, 'row', route)  20.5 us
    ppermute x4, starting transfers between devices, blocked_steps(): arrivals.append(lax.ppermute(own, ('row', 'col'), route))  11.4 us
    pallas_call x1, Pallas kernels, factor_of(): pl.pallas_call(factor_kernel, out_shape=jax.ShapeDtypeStruct((rank, rank)...  6.4 us
    pallas_call x1, Pallas kernels, core_of(): pl.pallas_call(core_kernel, out_shape=jax.ShapeDtypeStruct(inverse.shape,...  6.16 us
    pallas_call x2, Pallas kernels, product_part(): pl.pallas_call(functools.partial(product_kernel, counts=counts, places=pl...  4.8 us
  transfers between devices with their start and end apart: 25, of which 10 were waited for; matrix products, arithmetic and copies ran while one was open for 1% of the time, Pallas kernels for 20%

commit v1 on v0

--- a/solution.py
+++ b/solution.py
@@ -308,7 +308,7 @@
     *share_refs, out_ref, gram_ref = refs
     joined(where_ref, share_refs, gram_ref)
     rank = gram_ref.shape[0]
-    look = 4
+    look = 8
     bands = rank // 8
     sublanes = lax.broadcasted_iota(jnp.int32, (8, rank), 0)
     lanes = lax.broadcasted_iota(jnp.int32, (8, rank), 1)
@@ -387,13 +387,13 @@
         return contract(wide, twice, flat) + contract(left_high, right_low, flat)
 
     def newton(_, pair):
-        high, low = split_two(pair)
-        inner = product(high[rank:], low[rank:], high[:rank], low[:rank])
-        factor = 0.5 * (3.0 * identity - inner)
-        return product(high, low, *split_two(factor))
-
-    pair = jnp.concatenate([square / frobenius, identity], axis=0)
-    iterate = lax.fori_loop(0, NS_ITERS, newton, pair)[:rank]
+        iterate, partner = pair
+        iterate_parts, partner_parts = split_two(iterate), split_two(partner)
+        factor = 0.5 * (3.0 * identity - product(*partner_parts, *iterate_parts))
+        factor_parts = split_two(factor)
+        return product(*iterate_parts, *factor_parts), product(*factor_parts, *partner_parts)
+
+    iterate, _ = lax.fori_loop(0, NS_ITERS, newton, (square / frobenius, identity))
     root = jnp.sqrt(frobenius) * iterate
     response = (ritz + root) / (2.0 * penalty) - base_level * identity
     out_ref[...] = dot_three(dot_three(inverse, response, ((0,), (0,))), inverse)
@@ -558,7 +558,8 @@
         own = own + arrived
     half = [own]
     for s in range(1, n_col):
-        half.append(across_chips(own, s))
+        highest_step = 1 << (s.bit_length() - 1)
+        half.append(across_chips(half[s - highest_step], highest_step))
     arrivals = []
     for a in range(n_col):
         route = [

time: 150 us -> 144 us (0.960)
  waiting for transfers between devices: 26.7 us -> 24.6 us
  starting transfers between devices: 42.1 us -> 40.2 us
  Pallas kernels: 77.6 us -> 75.8 us
    ppermute x9, waiting for transfers between devices: 20.5 us -> 16.5 us  [across_chips(): return lax.ppermute(value, 'row', route)]
    ppermute x4, waiting for transfers between devices: 2.99 us -> 5.17 us  [blocked_steps(): arrivals.append(lax.ppermute(own, ('row', 'col'), route))]
    ppermute x9, starting transfers between devices: 24.9 us -> 23.2 us  [across_chips(): return lax.ppermute(value, 'row', route)]
    pallas_call x1, Pallas kernels: 6.4 us -> 4.69 us  [factor_of(): pl.pallas_call(factor_kernel, out_shape=jax.ShapeDtypeStruct((rank, rank)...]
  transfers between devices with their start and end apart: 25 -> 25, of which waited for: 10 -> 10; matrix products, arithmetic and copies ran while one was open for 1% -> 1% of each run, Pallas kernels for 20% -> 19%
where the time goes in v1:
time: 144 us
  Pallas kernels  75.8 us (53%)
  starting transfers between devices  40.2 us (28%)
  waiting for transfers between devices  24.6 us (17%)
  between operations  1.71 us (1%)
    pallas_call x3, Pallas kernels, image_part(): pl.pallas_call(image_kernel, out_shape=(jax.ShapeDtypeStruct((pieces, ran...  30 us
    pallas_call x1, Pallas kernels, finish(): pl.pallas_call(functools.partial(finish_kernel, groups=groups, pieces=pie...  28.7 us
    ppermute x9, starting transfers between devices, across_chips(): return lax.ppermute(value, 'row', route)  23.2 us
    ppermute x9, waiting for transfers between devices, across_chips(): return lax.ppermute(value, 'row', route)  16.5 us
    ppermute x4, starting transfers between devices, blocked_steps(): arrivals.append(lax.ppermute(own, ('row', 'col'), route))  11.1 us
    pallas_call x1, Pallas kernels, core_of(): pl.pallas_call(core_kernel, out_shape=jax.ShapeDtypeStruct(inverse.shape,...  6.02 us
    ppermute x4, waiting for transfers between devices, blocked_steps(): arrivals.append(lax.ppermute(own, ('row', 'col'), route))  5.17 us
    pallas_call x2, Pallas kernels, product_part(): pl.pallas_call(functools.partial(product_kernel, counts=counts, places=pl...  4.79 us
  transfers between devices with their start and end apart: 25, of which 10 were waited for; matrix products, arithmetic and copies ran while one was open for 1% of the time, Pallas kernels for 19%

profile of v1, /device:TPU:0, one launch (start us, length us, event | category | flops | bytes accessed | tf_op | source)
XLA Modules:
  0.0 143.8 jit_solution(12277576792764348168)
XLA Ops:
  1.0 11.7 %image_part.3 = (f32[3,128,512]{2,1,0:T(8,128)S(1)}, bf16[2048,1536]{1,0:T(8,128)(2,1)S(1)}, bf16[2048,1536]{1,0:T(8,128)(2,1)S(1)}, bf16[256,2048]{1,0:T(8,128)(2,1)S(1)}) custom-call(s32[3]{0:T(128)S(1)} %get-tuple-element.26.order_ref, bf16[2048,4096]{1,0:T(8,128)(2,1)} %est_ref.5, bf16[2048,4096]{1,0:T(8,128)(2,1)} %dual_ref.5, ...), custom_call_target="tpu_custom_call" | custom-call | tf_op jit(solution)/shard_map/image_part/pallas_call | solution.py:187
  12.7 0.6 collective-permute-start
  13.3 10.7 %image_part.4 = (f32[3,128,512]{2,1,0:T(8,128)S(1)}, bf16[2048,1536]{1,0:T(8,128)(2,1)S(1)}, bf16[2048,1536]{1,0:T(8,128)(2,1)S(1)}) custom-call(s32[3]{0:T(128)S(1)} %get-tuple-element.28.order_ref, bf16[2048,4096]{1,0:T(8,128)(2,1)} %est_ref.5, bf16[2048,4096]{1,0:T(8,128)(2,1)} %dual_ref.5, bf16[2048,4096]{1,0:T(8,128)(2,1)} %cov_ref.5, ...), custom_call_target="tpu_custom_call" | custom-call | tf_op jit(solution)/shard_map/image_part/pallas_call | solution.py:187
  24.2 2.5 %collective-permute-start.2 = (f32[128,512]{1,0:T(8,128)S(1)}, f32[128,512]{1,0:T(8,128)S(1)}, u32[]{:S(2)}, u32[]{:S(2)}) collective-permute-start(f32[128,512]{1,0:T(8,128)S(1)} %get-tuple-element.46), channel_id=1, source_target_pairs={{0,8},{4,12},{8,0},{12,4},{16,24},{20,28},{24,16},{28,20},{1,9},{5... | collective-permute-start | bytes 786440 | tf_op jit(solution)/shard_map/ppermute | solution.py:510
  26.7 1.5 %collective-permute-start.4 = (f32[128,512]{1,0:T(8,128)S(1)}, f32[128,512]{1,0:T(8,128)S(1)}, u32[]{:S(2)}, u32[]{:S(2)}) collective-permute-start(f32[128,512]{1,0:T(8,128)S(1)} %get-tuple-element.47), channel_id=1, source_target_pairs={{0,24},{4,28},{8,16},{12,20},{16,8},{20,12},{24,0},{28,4},{1,25},{... | collective-permute-start | bytes 786440 | tf_op jit(solution)/shard_map/ppermute | solution.py:510
  28.3 7.6 %image_part.5 = (f32[2,128,512]{2,1,0:T(8,128)S(1)}, bf16[2048,1024]{1,0:T(8,128)(2,1)S(1)}, bf16[2048,1024]{1,0:T(8,128)(2,1)S(1)}) custom-call(s32[2]{0:T(128)S(1)} %pad_add_fusion.2.order_ref, bf16[2048,4096]{1,0:T(8,128)(2,1)} %est_ref.5, bf16[2048,4096]{1,0:T(8,128)(2,1)} %dual_ref.5, bf16[2048,4096]{1,0:T(8,128)(2,1)} %cov_ref.5, ...), custom_call_target="tpu_custom_call" | custom-call | tf_op jit(solution)/shard_map/image_part/pallas_call | solution.py:187
  36.0 4.6 %collective-permute-done.4 = f32[128,512]{1,0:T(8,128)S(1)} collective-permute-done((f32[128,512]{1,0:T(8,128)S(1)}, f32[128,512]{1,0:T(8,128)S(1)}, u32[]{:S(2)}, u32[]{:S(2)}) %collective-permute-start.4) | collective-permute-done | bytes 262176 | tf_op jit(solution)/shard_map/ppermute | solution.py:510
  40.6 1.4 collective-permute-done.3
  42.1 1.6 %collective-permute-start.5 = (f32[128,512]{1,0:T(8,128)S(1)}, f32[128,512]{1,0:T(8,128)S(1)}, u32[]{:S(2)}, u32[]{:S(2)}) collective-permute-start(f32[128,512]{1,0:T(8,128)S(1)} %fusion.2.refs_5_), channel_id=1, source_target_pairs={{0,8},{4,12},{8,0},{12,4},{16,24},{20,28},{24,16},{28,20},{1,9},{5... | collective-permute-start | bytes 786440 | tf_op jit(solution)/shard_map/ppermute | solution.py:510
  44.2 5.3 %collective-permute-done.5.refs_2_ = f32[128,512]{1,0:T(8,128)S(1)} collective-permute-done((f32[128,512]{1,0:T(8,128)S(1)}, f32[128,512]{1,0:T(8,128)S(1)}, u32[]{:S(2)}, u32[]{:S(2)}) %collective-permute-start.5) | collective-permute-done | bytes 262176 | tf_op jit(solution)/shard_map/ppermute | solution.py:510
  49.5 0.6 collective-permute-start.9
  50.1 1.0 collective-permute-done.7.refs_3_
  51.0 5.5 %collective-permute-start.15 = (f32[128,512]{1,0:T(8,128)S(1)}, f32[128,512]{1,0:T(8,128)S(1)}, u32[]{:S(2)}, u32[]{:S(2)}) collective-permute-start(f32[128,512]{1,0:T(8,128)S(1)} %fusion.2.refs_5_), channel_id=1, source_target_pairs={{0,3},{1,11},{2,19},{4,7},{5,15},{6,23},{8,2},{9,10},{11,26},{12,6... | collective-permute-start | bytes 786440 | tf_op jit(solution)/shard_map/ppermute | solution.py:571
  56.6 2.8 %collective-permute-start.13 = (f32[128,512]{1,0:T(8,128)S(1)}, f32[128,512]{1,0:T(8,128)S(1)}, u32[]{:S(2)}, u32[]{:S(2)}) collective-permute-start(f32[128,512]{1,0:T(8,128)S(1)} %fusion.2.refs_5_), channel_id=1, source_target_pairs={{0,1},{2,17},{3,25},{4,5},{6,21},{7,29},{9,8},{10,16},{11,24},{13,... | collective-permute-start | bytes 786440 | tf_op jit(solution)/shard_map/ppermute | solution.py:571
  60.0 1.9 %collective-permute-start.14 = (f32[128,512]{1,0:T(8,128)S(1)}, f32[128,512]{1,0:T(8,128)S(1)}, u32[]{:S(2)}, u32[]{:S(2)}) collective-permute-start(f32[128,512]{1,0:T(8,128)S(1)} %fusion.2.refs_5_), channel_id=1, source_target_pairs={{0,2},{1,10},{3,26},{4,6},{5,14},{7,30},{8,3},{9,11},{10,19},{12,7... | collective-permute-start | bytes 786440 | tf_op jit(solution)/shard_map/ppermute | solution.py:571
  62.0 2.4 %product_part.2.refs_6_ = f32[2048,128]{1,0:T(8,128)S(1)} custom-call(bf16[2048,1536]{1,0:T(8,128)(2,1)S(1)} %get-tuple-element.37.refs_0_, bf16[2048,1024]{1,0:T(8,128)(2,1)S(1)} %get-tuple-element.34.refs_1_, f32[128,512]{1,0:T(8,128)S(1)} %collective-permute-done.5.refs_2_, f32[128,512]{1,0:T(8,128)S(1)} %collective-permute-done.7.refs_3_, ...), custom_call_target="tpu_custom_call" | custom-call | tf_op jit(solution)/shard_map/product_part/pallas_call | solution.py:238
  64.4 0.9 collective-permute-start.12
  65.3 2.4 %product_part.3.refs_4_ = f32[2048,128]{1,0:T(8,128)S(1)} custom-call(bf16[2048,1536]{1,0:T(8,128)(2,1)S(1)} %get-tuple-element.27.refs_0_, bf16[2048,1024]{1,0:T(8,128)(2,1)S(1)} %get-tuple-element.34.refs_1_, f32[128,512]{1,0:T(8,128)S(1)} %collective-permute-done.6.refs_2_, f32[128,512]{1,0:T(8,128)S(1)} %collective-permute-done.8.refs_3_, ...), custom_call_target="tpu_custom_call" | custom-call | tf_op jit(solution)/shard_map/product_part/pallas_call | solution.py:238
  68.9 5.2 %collective-permute-done.14 = f32[128,512]{1,0:T(8,128)S(1)} collective-permute-done((f32[128,512]{1,0:T(8,128)S(1)}, f32[128,512]{1,0:T(8,128)S(1)}, u32[]{:S(2)}, u32[]{:S(2)}) %collective-permute-start.14) | collective-permute-done | bytes 262176 | tf_op jit(solution)/shard_map/ppermute | solution.py:571
  74.2 1.5 %quadratic.1 = f32[2,2,64,128]{3,2,1,0:T(8,128)S(1)} custom-call(s32[5]{0:T(128)S(1)} %concatenate.8.where_ref, f32[128,512]{1,0:T(8,128)S(1)} %broadcast_select_fusion.3.refs_0_, f32[128,512]{1,0:T(8,128)S(1)} %broadcast_select_fusion.2.refs_1_, f32[128,512]{1,0:T(8,128)S(1)} %broadcast_select_fusion.1.refs_2_, ...), custom_call_target="tpu_custom_call" | custom-call | tf_op jit(solution)/shard_map/quadratic/pallas_call | solution.py:280
  76.0 1.1 collective-permute-done.16
  77.1 6.9 %collective-permute-start.19 = (f32[2,64,128]{2,1,0:T(8,128)S(1)}, f32[2,64,128]{2,1,0:T(8,128)S(1)}, u32[]{:S(2)}, u32[]{:S(2)}) collective-permute-start(f32[2,64,128]{2,1,0:T(8,128)S(1)} %fusion.3), channel_id=1, source_target_pairs={{0,24},{4,28},{8,16},{12,20},{16,8},{20,12},{24,0},{28,4},{1,25},{... | collective-permute-start | bytes 196616 | tf_op jit(solution)/shard_map/ppermute | solution.py:510
  84.0 9.5 %collective-permute-start.18 = (f32[2,64,128]{2,1,0:T(8,128)S(1)}, f32[2,64,128]{2,1,0:T(8,128)S(1)}, u32[]{:S(2)}, u32[]{:S(2)}) collective-permute-start(f32[2,64,128]{2,1,0:T(8,128)S(1)} %fusion.3), channel_id=1, source_target_pairs={{0,16},{4,20},{8,24},{12,28},{16,0},{20,4},{24,8},{28,12},{1,17},{... | collective-permute-start | bytes 196616 | tf_op jit(solution)/shard_map/ppermute | solution.py:510
  93.6 2.2 %collective-permute-done.18 = f32[2,64,128]{2,1,0:T(8,128)S(1)} collective-permute-done((f32[2,64,128]{2,1,0:T(8,128)S(1)}, f32[2,64,128]{2,1,0:T(8,128)S(1)}, u32[]{:S(2)}, u32[]{:S(2)}) %collective-permute-start.18) | collective-permute-done | bytes 65568 | tf_op jit(solution)/shard_map/ppermute | solution.py:510
  95.8 2.0 %collective-permute-done.17 = f32[2,64,128]{2,1,0:T(8,128)S(1)} collective-permute-done((f32[2,64,128]{2,1,0:T(8,128)S(1)}, f32[2,64,128]{2,1,0:T(8,128)S(1)}, u32[]{:S(2)}, u32[]{:S(2)}) %collective-permute-start.17) | collective-permute-done | bytes 65568 | tf_op jit(solution)/shard_map/ppermute | solution.py:510
  97.8 0.5 collective-permute-start.23
  98.4 3.9 %collective-permute-start.21 = (f32[64,128]{1,0:T(8,128)S(1)}, f32[64,128]{1,0:T(8,128)S(1)}, u32[]{:S(2)}, u32[]{:S(2)}) collective-permute-start(f32[64,128]{1,0:T(8,128)S(1)} %get-tuple-element.42), channel_id=1, source_target_pairs={{0,1},{1,0},{2,3},{3,2},{4,5},{5,4},{6,7},{7,6},{8,9},{9,8},{10,11... | collective-permute-start | bytes 98312 | tf_op jit(solution)/shard_map/ppermute | solution.py:513
  102.4 1.2 collective-permute-done.23
  103.6 0.6 collective-permute-done.21
  104.4 4.7 %factor.1.inverse_ref = f32[128,128]{1,0:T(8,128)S(1)} custom-call(s32[5]{0:T(128)S(1)} %concatenate.8.where_ref, f32[64,128]{1,0:T(8,128)S(1)} %get-tuple-element.41.refs_0_, f32[64,128]{1,0:T(8,128)S(1)} %collective-permute-done.20.refs_1_), custom_call_target="tpu_custom_call" | custom-call | tf_op jit(solution)/shard_map/factor/pallas_call | solution.py:359
  109.1 6.0 %core.1.core_ref = f32[128,128]{1,0:T(8,128)S(1)} custom-call(s32[5]{0:T(128)S(1)} %concatenate.8.where_ref, f32[128,128]{1,0:T(8,128)S(1)} %factor.1.inverse_ref, f32[64,128]{1,0:T(8,128)S(1)} %add_add_fusion.1.refs_0_, f32[64,128]{1,0:T(8,128)S(1)} %collective-permute-done.24.refs_1_), custom_call_target="tpu_custom_call" | custom-call | tf_op jit(solution)/shard_map/core/pallas_call | solution.py:404
  115.1 28.7 %finish.1 = (f32[2048,4096]{1,0:T(8,128)}, bf16[2048,4096]{1,0:T(8,128)(2,1)}) custom-call(s32[18]{0:T(128)S(1)} %concatenate.9.place_ref, f32[4,128,512]{2,1,0:T(8,128)S(1)} %pad_maximum_fusion.left_ref, f32[128,128]{1,0:T(8,128)S(1)} %core.1.core_ref, f32[8,128,512]{2,1,0:T(8,128)S(1)} %bitcast_dynamic-update-slice_fusion.right_ref, ...), custom_call_target="tpu_custom_call" | custom-call | tf_op jit(solution)/shard_map/finish/pallas_call | solution.py:463
  (55 shorter events, 3.1 us)
Async XLA Ops:
  12.7 11.3 %collective-permute-start = (f32[3,128,512]{2,1,0:T(8,128)S(1)}, f32[3,128,512]{2,1,0:T(8,128)S(1)}, u32[]{:S(2)}, u32[]{:S(2)}) collective-permute-start(f32[3,128,512]{2,1,0:T(8,128)S(1)} %get-tuple-element.31), channel_id=1, source_target_pairs={{0,4},{4,0},{8,12},{12,8},{16,20},{20,16},{24,28},{28,24},{1,5},{5... | collective-permute-start | bytes 2359304 | tf_op jit(solution)/shard_map/ppermute | solution.py:506
  24.2 11.8 %collective-permute-start.2 = (f32[128,512]{1,0:T(8,128)S(1)}, f32[128,512]{1,0:T(8,128)S(1)}, u32[]{:S(2)}, u32[]{:S(2)}) collective-permute-start(f32[128,512]{1,0:T(8,128)S(1)} %get-tuple-element.46), channel_id=1, source_target_pairs={{0,8},{4,12},{8,0},{12,4},{16,24},{20,28},{24,16},{28,20},{1,9},{5... | collective-permute-start | bytes 786440 | tf_op jit(solution)/shard_map/ppermute | solution.py:510
  26.7 13.9 %collective-permute-start.4 = (f32[128,512]{1,0:T(8,128)S(1)}, f32[128,512]{1,0:T(8,128)S(1)}, u32[]{:S(2)}, u32[]{:S(2)}) collective-permute-start(f32[128,512]{1,0:T(8,128)S(1)} %get-tuple-element.47), channel_id=1, source_target_pairs={{0,24},{4,28},{8,16},{12,20},{16,8},{20,12},{24,0},{28,4},{1,25},{... | collective-permute-start | bytes 786440 | tf_op jit(solution)/shard_map/ppermute | solution.py:510
  28.2 13.8 %collective-permute-start.3 = (f32[128,512]{1,0:T(8,128)S(1)}, f32[128,512]{1,0:T(8,128)S(1)}, u32[]{:S(2)}, u32[]{:S(2)}) collective-permute-start(f32[128,512]{1,0:T(8,128)S(1)} %get-tuple-element.48), channel_id=1, source_target_pairs={{0,16},{4,20},{8,24},{12,28},{16,0},{20,4},{24,8},{28,12},{1,17},{... | collective-permute-start | bytes 786440 | tf_op jit(solution)/shard_map/ppermute | solution.py:510
  35.9 6.1 %collective-permute-start.1 = (f32[128,512]{1,0:T(8,128)S(1)}, f32[128,512]{1,0:T(8,128)S(1)}, u32[]{:S(2)}, u32[]{:S(2)}) collective-permute-start(f32[128,512]{1,0:T(8,128)S(1)} %slice_bitcast_fusion.3), channel_id=1, source_target_pairs={{0,4},{4,0},{8,12},{12,8},{16,20},{20,16},{24,28},{28,24},{1,5},{5... | collective-permute-start | bytes 786440 | tf_op jit(solution)/shard_map/ppermute | solution.py:506
  42.1 7.3 %collective-permute-start.5 = (f32[128,512]{1,0:T(8,128)S(1)}, f32[128,512]{1,0:T(8,128)S(1)}, u32[]{:S(2)}, u32[]{:S(2)}) collective-permute-start(f32[128,512]{1,0:T(8,128)S(1)} %fusion.2.refs_5_), channel_id=1, source_target_pairs={{0,8},{4,12},{8,0},{12,4},{16,24},{20,28},{24,16},{28,20},{1,9},{5... | collective-permute-start | bytes 786440 | tf_op jit(solution)/shard_map/ppermute | solution.py:510
  43.7 7.4 %collective-permute-start.7 = (f32[128,512]{1,0:T(8,128)S(1)}, f32[128,512]{1,0:T(8,128)S(1)}, u32[]{:S(2)}, u32[]{:S(2)}) collective-permute-start(f32[128,512]{1,0:T(8,128)S(1)} %fusion.2.refs_5_), channel_id=1, source_target_pairs={{0,16},{4,20},{8,24},{12,28},{16,0},{20,4},{24,8},{28,12},{1,17},{... | collective-permute-start | bytes 786440 | tf_op jit(solution)/shard_map/ppermute | solution.py:510
  49.5 10.0 %collective-permute-start.9 = (f32[128,512]{1,0:T(8,128)S(1)}, f32[128,512]{1,0:T(8,128)S(1)}, u32[]{:S(2)}, u32[]{:S(2)}) collective-permute-start(f32[128,512]{1,0:T(8,128)S(1)} %collective-permute-done.5.refs_2_), channel_id=1, source_target_pairs={{0,16},{4,20},{8,24},{12,28},{16,0},{20,4},{24,8},{28,12},{1,17},{... | collective-permute-start | bytes 786440 | tf_op jit(solution)/shard_map/ppermute | solution.py:510
  50.1 9.4 %collective-permute-start.6 = (f32[128,512]{1,0:T(8,128)S(1)}, f32[128,512]{1,0:T(8,128)S(1)}, u32[]{:S(2)}, u32[]{:S(2)}) collective-permute-start(f32[128,512]{1,0:T(8,128)S(1)} %collective-permute-done.5.refs_2_), channel_id=1, source_target_pairs={{0,4},{4,0},{8,12},{12,8},{16,20},{20,16},{24,28},{28,24},{1,5},{5... | collective-permute-start | bytes 786440 | tf_op jit(solution)/shard_map/ppermute | solution.py:506
  51.0 9.0 %collective-permute-start.8 = (f32[128,512]{1,0:T(8,128)S(1)}, f32[128,512]{1,0:T(8,128)S(1)}, u32[]{:S(2)}, u32[]{:S(2)}) collective-permute-start(f32[128,512]{1,0:T(8,128)S(1)} %collective-permute-done.7.refs_3_), channel_id=1, source_target_pairs={{0,4},{4,0},{8,12},{12,8},{16,20},{20,16},{24,28},{28,24},{1,5},{5... | collective-permute-start | bytes 786440 | tf_op jit(solution)/shard_map/ppermute | solution.py:506
  51.0 23.1 %collective-permute-start.15 = (f32[128,512]{1,0:T(8,128)S(1)}, f32[128,512]{1,0:T(8,128)S(1)}, u32[]{:S(2)}, u32[]{:S(2)}) collective-permute-start(f32[128,512]{1,0:T(8,128)S(1)} %fusion.2.refs_5_), channel_id=1, source_target_pairs={{0,3},{1,11},{2,19},{4,7},{5,15},{6,23},{8,2},{9,10},{11,26},{12,6... | collective-permute-start | bytes 786440 | tf_op jit(solution)/shard_map/ppermute | solution.py:571
  56.6 12.3 %collective-permute-start.13 = (f32[128,512]{1,0:T(8,128)S(1)}, f32[128,512]{1,0:T(8,128)S(1)}, u32[]{:S(2)}, u32[]{:S(2)}) collective-permute-start(f32[128,512]{1,0:T(8,128)S(1)} %fusion.2.refs_5_), channel_id=1, source_target_pairs={{0,1},{2,17},{3,25},{4,5},{6,21},{7,29},{9,8},{10,16},{11,24},{13,... | collective-permute-start | bytes 786440 | tf_op jit(solution)/shard_map/ppermute | solution.py:571
  59.4 5.0 %collective-permute-start.11 = (f32[128,512]{1,0:T(8,128)S(1)}, f32[128,512]{1,0:T(8,128)S(1)}, u32[]{:S(2)}, u32[]{:S(2)}) collective-permute-start(f32[128,512]{1,0:T(8,128)S(1)} %fusion.2.refs_5_), channel_id=1, source_target_pairs={{0,4},{4,0},{8,12},{12,8},{16,20},{20,16},{24,28},{28,24},{1,5},{5... | collective-permute-start | bytes 786440 | tf_op jit(solution)/shard_map/ppermute | solution.py:506
  59.5 5.8 %collective-permute-start.10 = (f32[128,512]{1,0:T(8,128)S(1)}, f32[128,512]{1,0:T(8,128)S(1)}, u32[]{:S(2)}, u32[]{:S(2)}) collective-permute-start(f32[128,512]{1,0:T(8,128)S(1)} %collective-permute-done.9.refs_4_), channel_id=1, source_target_pairs={{0,4},{4,0},{8,12},{12,8},{16,20},{20,16},{24,28},{28,24},{1,5},{5... | collective-permute-start | bytes 786440 | tf_op jit(solution)/shard_map/ppermute | solution.py:506
  60.0 14.0 %collective-permute-start.14 = (f32[128,512]{1,0:T(8,128)S(1)}, f32[128,512]{1,0:T(8,128)S(1)}, u32[]{:S(2)}, u32[]{:S(2)}) collective-permute-start(f32[128,512]{1,0:T(8,128)S(1)} %fusion.2.refs_5_), channel_id=1, source_target_pairs={{0,2},{1,10},{3,26},{4,6},{5,14},{7,30},{8,3},{9,11},{10,19},{12,7... | collective-permute-start | bytes 786440 | tf_op jit(solution)/shard_map/ppermute | solution.py:571
  64.4 9.8 %collective-permute-start.12 = (f32[128,512]{1,0:T(8,128)S(1)}, f32[128,512]{1,0:T(8,128)S(1)}, u32[]{:S(2)}, u32[]{:S(2)}) collective-permute-start(f32[128,512]{1,0:T(8,128)S(1)} %fusion.2.refs_5_), channel_id=1, source_target_pairs={{1,8},{2,16},{3,24},{5,12},{6,20},{7,28},{8,1},{10,17},{11,25},{12... | collective-permute-start | bytes 786440 | tf_op jit(solution)/shard_map/ppermute | solution.py:571
  75.8 1.3 collective-permute-start.16
  77.1 16.4 %collective-permute-start.19 = (f32[2,64,128]{2,1,0:T(8,128)S(1)}, f32[2,64,128]{2,1,0:T(8,128)S(1)}, u32[]{:S(2)}, u32[]{:S(2)}) collective-permute-start(f32[2,64,128]{2,1,0:T(8,128)S(1)} %fusion.3), channel_id=1, source_target_pairs={{0,24},{4,28},{8,16},{12,20},{16,8},{20,12},{24,0},{28,4},{1,25},{... | collective-permute-start | bytes 196616 | tf_op jit(solution)/shard_map/ppermute | solution.py:510
  84.0 11.8 %collective-permute-start.18 = (f32[2,64,128]{2,1,0:T(8,128)S(1)}, f32[2,64,128]{2,1,0:T(8,128)S(1)}, u32[]{:S(2)}, u32[]{:S(2)}) collective-permute-start(f32[2,64,128]{2,1,0:T(8,128)S(1)} %fusion.3), channel_id=1, source_target_pairs={{0,16},{4,20},{8,24},{12,28},{16,0},{20,4},{24,8},{28,12},{1,17},{... | collective-permute-start | bytes 196616 | tf_op jit(solution)/shard_map/ppermute | solution.py:510
  93.5 4.3 %collective-permute-start.17 = (f32[2,64,128]{2,1,0:T(8,128)S(1)}, f32[2,64,128]{2,1,0:T(8,128)S(1)}, u32[]{:S(2)}, u32[]{:S(2)}) collective-permute-start(f32[2,64,128]{2,1,0:T(8,128)S(1)} %fusion.3), channel_id=1, source_target_pairs={{0,8},{4,12},{8,0},{12,4},{16,24},{20,28},{24,16},{28,20},{1,9},{5... | collective-permute-start | bytes 196616 | tf_op jit(solution)/shard_map/ppermute | solution.py:510
  97.8 5.8 %collective-permute-start.23 = (f32[64,128]{1,0:T(8,128)S(1)}, f32[64,128]{1,0:T(8,128)S(1)}, u32[]{:S(2)}, u32[]{:S(2)}) collective-permute-start(f32[64,128]{1,0:T(8,128)S(1)} %get-tuple-element.42), channel_id=1, source_target_pairs={{0,3},{1,2},{2,1},{3,0},{4,7},{5,6},{6,5},{7,4},{8,11},{9,10},{10,... | collective-permute-start | bytes 98312 | tf_op jit(solution)/shard_map/ppermute | solution.py:513
  98.4 5.2 %collective-permute-start.22 = (f32[64,128]{1,0:T(8,128)S(1)}, f32[64,128]{1,0:T(8,128)S(1)}, u32[]{:S(2)}, u32[]{:S(2)}) collective-permute-start(f32[64,128]{1,0:T(8,128)S(1)} %get-tuple-element.42), channel_id=1, source_target_pairs={{0,2},{1,3},{2,0},{3,1},{4,6},{5,7},{6,4},{7,5},{8,10},{9,11},{10,... | collective-permute-start | bytes 98312 | tf_op jit(solution)/shard_map/ppermute | solution.py:513
  98.4 5.8 %collective-permute-start.21 = (f32[64,128]{1,0:T(8,128)S(1)}, f32[64,128]{1,0:T(8,128)S(1)}, u32[]{:S(2)}, u32[]{:S(2)}) collective-permute-start(f32[64,128]{1,0:T(8,128)S(1)} %get-tuple-element.42), channel_id=1, source_target_pairs={{0,1},{1,0},{2,3},{3,2},{4,5},{5,4},{6,7},{7,6},{8,9},{9,8},{10,11... | collective-permute-start | bytes 98312 | tf_op jit(solution)/shard_map/ppermute | solution.py:513
  102.3 2.0 %collective-permute-start.20 = (f32[64,128]{1,0:T(8,128)S(1)}, f32[64,128]{1,0:T(8,128)S(1)}, u32[]{:S(2)}, u32[]{:S(2)}) collective-permute-start(f32[64,128]{1,0:T(8,128)S(1)} %get-tuple-element.41.refs_0_), channel_id=1, source_target_pairs={{0,4},{4,0},{8,12},{12,8},{16,20},{20,16},{24,28},{28,24},{1,5},{5... | collective-permute-start | bytes 98312 | tf_op jit(solution)/shard_map/ppermute | solution.py:506
  104.2 4.9 %collective-permute-start.24 = (f32[64,128]{1,0:T(8,128)S(1)}, f32[64,128]{1,0:T(8,128)S(1)}, u32[]{:S(2)}, u32[]{:S(2)}) collective-permute-start(f32[64,128]{1,0:T(8,128)S(1)} %add_add_fusion.1.refs_0_), channel_id=1, source_target_pairs={{0,4},{4,0},{8,12},{12,8},{16,20},{20,16},{24,28},{28,24},{1,5},{5... | collective-permute-start | bytes 98312 | tf_op jit(solution)/shard_map/ppermute | solution.py:506

commit v2 on v1

--- a/solution.py
+++ b/solution.py
@@ -258,34 +258,37 @@
 
 def quadratic_kernel(where_ref, *refs):
     *piece_refs, product_ref, out_ref, small_ref, gram_ref = refs
+    count = len(piece_refs) // 2
     rank, width = piece_refs[0].shape
     small = jnp.zeros((rank, rank), jnp.float32)
     gram = jnp.zeros((rank, rank), jnp.float32)
-    for index, piece_ref in enumerate(piece_refs):
+    own_block = where_ref[count + 1] > 0
+    for index in range(count):
         start = pl.multiple_of(where_ref[index] * width, width)
-        small += dot_three(piece_ref[...], product_ref[pl.ds(start, width), :])
-        gram += dot_three(piece_ref[...], piece_ref[...], ((1,), (1,)))
+        piece = jnp.where(own_block, piece_refs[index][...], piece_refs[count + index][...])
+        small += dot_three(piece, product_ref[pl.ds(start, width), :])
+        gram += dot_three(piece, piece, ((1,), (1,)))
     small_ref[...] = small
     gram_ref[...] = gram
     lanes, _, share, _ = out_ref.shape
     for step in range(lanes):
-        start = pl.multiple_of((where_ref[len(piece_refs)] ^ step) * share, share)
+        start = pl.multiple_of((where_ref[count] ^ step) * share, share)
         out_ref[step, 0] = small_ref[pl.ds(start, share), :]
         out_ref[step, 1] = gram_ref[pl.ds(start, share), :]
 
 
-def quadratic(order, pieces, product, lanes):
+def quadratic(order, here, arrived, product, lanes):
     rank = product.shape[1]
     vmem = pl.BlockSpec(memory_space=pltpu.VMEM)
     return pl.pallas_call(
         quadratic_kernel,
         out_shape=jax.ShapeDtypeStruct((lanes, 2, rank // lanes, rank), jnp.float32),
-        in_specs=[pl.BlockSpec(memory_space=pltpu.SMEM)] + [vmem] * (len(pieces) + 1),
+        in_specs=[pl.BlockSpec(memory_space=pltpu.SMEM)] + [vmem] * (2 * len(here) + 1),
         out_specs=vmem,
         scratch_shapes=[pltpu.VMEM((rank, rank), jnp.float32)] * 2,
         compiler_params=pltpu.CompilerParams(vmem_limit_bytes=8 * 2**20),
         name="quadratic",
-    )(order, *pieces, product)
+    )(order, *here, *arrived, product)
 
 
 def joined(where_ref, share_refs, whole_ref):
@@ -528,8 +531,11 @@
     corner = jnp.stack([row_index * rows, col_index * columns]).astype(jnp.int32)
     place = jnp.concatenate(orders + [piece_rows, piece_rows, corner])
     piece_rows = jnp.concatenate([piece_rows, lane.reshape(1).astype(jnp.int32)])
-    local = jnp.broadcast_to(chip == col_index, (8, 128)).astype(jnp.float32)
-    orders, piece_rows, place, local = lax.optimization_barrier((orders, piece_rows, place, local))
+    local = jnp.broadcast_to(chip == col_index, (1, 1)).astype(jnp.float32)
+    spots = jnp.concatenate([piece_rows, (chip == col_index).reshape(1).astype(jnp.int32)])
+    orders, piece_rows, place, local, spots = lax.optimization_barrier(
+        (orders, piece_rows, place, local, spots)
+    )
 
     part, high, held, basis = {}, [], [], in_hbm(start_basis)
     for index, call in enumerate(calls):
@@ -583,12 +589,11 @@
             [right[step, s] for s in range(1, n_col)] + [right[step, 0]],
             product,
         )
-    local, product = lax.optimization_barrier((local, product))
-    left = [jnp.where(local[:1, :1] > 0.5, half[a], arrivals[a]) for a in range(n_col)]
-    shares = quadratic(piece_rows, left, product, lanes)
+    shares = quadratic(spots, half, arrivals, product, lanes)
     both = sum([across_lanes(shares[step], step) for step in range(1, lanes)], shares[0])
     both = total_of(both, across_chips, n_col)
-    small, gram = lax.optimization_barrier((both[0], both[1]))
+    small, gram, local = lax.optimization_barrier((both[0], both[1], local))
+    left = [jnp.where(local > 0.5, half[a], arrivals[a]) for a in range(n_col)]
 
     def of_lanes(share):
         return [share] + [across_lanes(share, step) for step in range(1, lanes)]

time: 144 us -> 144 us (level)
  transfers between devices with their start and end apart: 25 -> 25, of which waited for: 10 -> 11; matrix products, arithmetic and copies ran while one was open for 1% -> 0% of each run, Pallas kernels for 19% -> 19%
where the time goes in v2:
time: 144 us
  Pallas kernels  75.7 us (53%)
  starting transfers between devices  41.1 us (29%)
  waiting for transfers between devices  24.6 us (17%)
    pallas_call x3, Pallas kernels, image_part(): pl.pallas_call(image_kernel, out_shape=(jax.ShapeDtypeStruct((pieces, ran...  30 us
    pallas_call x1, Pallas kernels, finish(): pl.pallas_call(functools.partial(finish_kernel, groups=groups, pieces=pie...  28.6 us
    ppermute x9, starting transfers between devices, across_chips(): return lax.ppermute(value, 'row', route)  23.9 us
    ppermute x9, waiting for transfers between devices, across_chips(): return lax.ppermute(value, 'row', route)  15.1 us
    ppermute x4, starting transfers between devices, blocked_steps(): arrivals.append(lax.ppermute(own, ('row', 'col'), route))  11.7 us
    ppermute x4, waiting for transfers between devices, blocked_steps(): arrivals.append(lax.ppermute(own, ('row', 'col'), route))  6.1 us
    pallas_call x1, Pallas kernels, core_of(): pl.pallas_call(core_kernel, out_shape=jax.ShapeDtypeStruct(inverse.shape,...  6.02 us
    pallas_call x2, Pallas kernels, product_part(): pl.pallas_call(functools.partial(product_kernel, counts=counts, places=pl...  4.77 us
  transfers between devices with their start and end apart: 25, of which 11 were waited for; matrix products, arithmetic and copies ran while one was open for 0% of the time, Pallas kernels for 19%

profile of v2, /device:TPU:0, one launch (start us, length us, event | category | flops | bytes accessed | tf_op | source)
XLA Modules:
  0.0 143.5 jit_solution(6439390550665191064)
XLA Ops:
  1.1 11.7 %image_part.3 = (f32[3,128,512]{2,1,0:T(8,128)S(1)}, bf16[2048,1536]{1,0:T(8,128)(2,1)S(1)}, bf16[2048,1536]{1,0:T(8,128)(2,1)S(1)}, bf16[256,2048]{1,0:T(8,128)(2,1)S(1)}) custom-call(s32[3]{0:T(128)S(1)} %get-tuple-element.27.order_ref, bf16[2048,4096]{1,0:T(8,128)(2,1)} %est_ref.5, bf16[2048,4096]{1,0:T(8,128)(2,1)} %dual_ref.5, ...), custom_call_target="tpu_custom_call" | custom-call | tf_op jit(solution)/shard_map/image_part/pallas_call | solution.py:187
  13.4 10.7 %image_part.4 = (f32[3,128,512]{2,1,0:T(8,128)S(1)}, bf16[2048,1536]{1,0:T(8,128)(2,1)S(1)}, bf16[2048,1536]{1,0:T(8,128)(2,1)S(1)}) custom-call(s32[3]{0:T(128)S(1)} %get-tuple-element.26.order_ref, bf16[2048,4096]{1,0:T(8,128)(2,1)} %est_ref.5, bf16[2048,4096]{1,0:T(8,128)(2,1)} %dual_ref.5, bf16[2048,4096]{1,0:T(8,128)(2,1)} %cov_ref.5, ...), custom_call_target="tpu_custom_call" | custom-call | tf_op jit(solution)/shard_map/image_part/pallas_call | solution.py:187
  24.3 2.5 %collective-permute-start.2 = (f32[128,512]{1,0:T(8,128)S(1)}, f32[128,512]{1,0:T(8,128)S(1)}, u32[]{:S(2)}, u32[]{:S(2)}) collective-permute-start(f32[128,512]{1,0:T(8,128)S(1)} %get-tuple-element.46), channel_id=1, source_target_pairs={{0,8},{4,12},{8,0},{12,4},{16,24},{20,28},{24,16},{28,20},{1,9},{5... | collective-permute-start | bytes 786440 | tf_op jit(solution)/shard_map/ppermute | solution.py:513
  26.8 1.5 %collective-permute-start.4 = (f32[128,512]{1,0:T(8,128)S(1)}, f32[128,512]{1,0:T(8,128)S(1)}, u32[]{:S(2)}, u32[]{:S(2)}) collective-permute-start(f32[128,512]{1,0:T(8,128)S(1)} %get-tuple-element.47), channel_id=1, source_target_pairs={{0,24},{4,28},{8,16},{12,20},{16,8},{20,12},{24,0},{28,4},{1,25},{... | collective-permute-start | bytes 786440 | tf_op jit(solution)/shard_map/ppermute | solution.py:513
  28.4 7.6 %image_part.5 = (f32[2,128,512]{2,1,0:T(8,128)S(1)}, bf16[2048,1024]{1,0:T(8,128)(2,1)S(1)}, bf16[2048,1024]{1,0:T(8,128)(2,1)S(1)}) custom-call(s32[2]{0:T(128)S(1)} %pad_add_fusion.2.order_ref, bf16[2048,4096]{1,0:T(8,128)(2,1)} %est_ref.5, bf16[2048,4096]{1,0:T(8,128)(2,1)} %dual_ref.5, bf16[2048,4096]{1,0:T(8,128)(2,1)} %cov_ref.5, ...), custom_call_target="tpu_custom_call" | custom-call | tf_op jit(solution)/shard_map/image_part/pallas_call | solution.py:187
  36.1 4.6 %collective-permute-done.4 = f32[128,512]{1,0:T(8,128)S(1)} collective-permute-done((f32[128,512]{1,0:T(8,128)S(1)}, f32[128,512]{1,0:T(8,128)S(1)}, u32[]{:S(2)}, u32[]{:S(2)}) %collective-permute-start.4) | collective-permute-done | bytes 262176 | tf_op jit(solution)/shard_map/ppermute | solution.py:513
  40.7 1.4 collective-permute-done.3
  42.6 1.7 %collective-permute-start.5 = (f32[128,512]{1,0:T(8,128)S(1)}, f32[128,512]{1,0:T(8,128)S(1)}, u32[]{:S(2)}, u32[]{:S(2)}) collective-permute-start(f32[128,512]{1,0:T(8,128)S(1)} %fusion.2.refs_5_.refs_0_), channel_id=1, source_target_pairs={{0,8},{4,12},{8,0},{12,4},{16,24},{20,28},{24,16},{28,20},{1,9},{5... | collective-permute-start | bytes 786440 | tf_op jit(solution)/shard_map/ppermute | solution.py:513
  44.3 5.3 %collective-permute-done.6.refs_3_.refs_2_ = f32[128,512]{1,0:T(8,128)S(1)} collective-permute-done((f32[128,512]{1,0:T(8,128)S(1)}, f32[128,512]{1,0:T(8,128)S(1)}, u32[]{:S(2)}, u32[]{:S(2)}) %collective-permute-start.6) | collective-permute-done | bytes 262176 | tf_op jit(solution)/shard_map/ppermute | solution.py:513
  50.0 1.2 collective-permute-start.7
  51.3 5.5 %collective-permute-start.11 = (f32[128,512]{1,0:T(8,128)S(1)}, f32[128,512]{1,0:T(8,128)S(1)}, u32[]{:S(2)}, u32[]{:S(2)}) collective-permute-start(f32[128,512]{1,0:T(8,128)S(1)} %fusion.2.refs_5_.refs_0_), channel_id=1, source_target_pairs={{0,3},{1,11},{2,19},{4,7},{5,15},{6,23},{8,2},{9,10},{11,26},{12,6... | collective-permute-start | bytes 786440 | tf_op jit(solution)/shard_map/ppermute | solution.py:577
  56.8 2.7 %collective-permute-start.10 = (f32[128,512]{1,0:T(8,128)S(1)}, f32[128,512]{1,0:T(8,128)S(1)}, u32[]{:S(2)}, u32[]{:S(2)}) collective-permute-start(f32[128,512]{1,0:T(8,128)S(1)} %fusion.2.refs_5_.refs_0_), channel_id=1, source_target_pairs={{0,2},{1,10},{3,26},{4,6},{5,14},{7,30},{8,3},{9,11},{10,19},{12,7... | collective-permute-start | bytes 786440 | tf_op jit(solution)/shard_map/ppermute | solution.py:577
  59.5 2.6 %collective-permute-start.9 = (f32[128,512]{1,0:T(8,128)S(1)}, f32[128,512]{1,0:T(8,128)S(1)}, u32[]{:S(2)}, u32[]{:S(2)}) collective-permute-start(f32[128,512]{1,0:T(8,128)S(1)} %fusion.2.refs_5_.refs_0_), channel_id=1, source_target_pairs={{0,1},{2,17},{3,25},{4,5},{6,21},{7,29},{9,8},{10,16},{11,24},{13,... | collective-permute-start | bytes 786440 | tf_op jit(solution)/shard_map/ppermute | solution.py:577
  62.1 0.9 collective-permute-start.8
  63.1 2.4 %product_part.2.refs_6_ = f32[2048,128]{1,0:T(8,128)S(1)} custom-call(bf16[2048,1536]{1,0:T(8,128)(2,1)S(1)} %get-tuple-element.37.refs_0_, bf16[2048,1024]{1,0:T(8,128)(2,1)S(1)} %get-tuple-element.36.refs_1_, f32[128,512]{1,0:T(8,128)S(1)} %collective-permute-done.5.refs_2_.refs_1_, f32[128,512]{1,0:T(8,128)S(1)} %collective-permute-done.6.refs_3_.refs_2_, ...), custom_call_target="tpu_custom_call" | custom-call | tf_op jit(solution)/shard_map/product_part/pallas_call | solution.py:238
  65.6 2.4 %product_part.3.refs_8_ = f32[2048,128]{1,0:T(8,128)S(1)} custom-call(bf16[2048,1536]{1,0:T(8,128)(2,1)S(1)} %get-tuple-element.35.refs_0_, bf16[2048,1024]{1,0:T(8,128)(2,1)S(1)} %get-tuple-element.36.refs_1_, f32[128,512]{1,0:T(8,128)S(1)} %collective-permute-done.12.refs_2_, f32[128,512]{1,0:T(8,128)S(1)} %collective-permute-done.13.refs_3_, ...), custom_call_target="tpu_custom_call" | custom-call | tf_op jit(solution)/shard_map/product_part/pallas_call | solution.py:238
  68.0 1.2 collective-permute-done.10.refs_6_
  69.2 4.9 %collective-permute-done.9.refs_5_ = f32[128,512]{1,0:T(8,128)S(1)} collective-permute-done((f32[128,512]{1,0:T(8,128)S(1)}, f32[128,512]{1,0:T(8,128)S(1)}, u32[]{:S(2)}, u32[]{:S(2)}) %collective-permute-start.9) | collective-permute-done | bytes 262176 | tf_op jit(solution)/shard_map/ppermute | solution.py:577
  74.0 1.5 %quadratic.1 = f32[2,2,64,128]{3,2,1,0:T(8,128)S(1)} custom-call(s32[6]{0:T(128)S(1)} %concatenate.14.where_ref, f32[128,512]{1,0:T(8,128)S(1)} %fusion.2.refs_5_.refs_0_, f32[128,512]{1,0:T(8,128)S(1)} %collective-permute-done.5.refs_2_.refs_1_, f32[128,512]{1,0:T(8,128)S(1)} %collective-permute-done.6.refs_3_.refs_2_, ...), custom_call_target="tpu_custom_call" | custom-call | tf_op jit(solution)/shard_map/quadratic/pallas_call | solution.py:283
  75.8 1.1 collective-permute-done.16
  76.9 8.4 %collective-permute-start.19 = (f32[2,64,128]{2,1,0:T(8,128)S(1)}, f32[2,64,128]{2,1,0:T(8,128)S(1)}, u32[]{:S(2)}, u32[]{:S(2)}) collective-permute-start(f32[2,64,128]{2,1,0:T(8,128)S(1)} %fusion.3), channel_id=1, source_target_pairs={{0,24},{4,28},{8,16},{12,20},{16,8},{20,12},{24,0},{28,4},{1,25},{... | collective-permute-start | bytes 196616 | tf_op jit(solution)/shard_map/ppermute | solution.py:513
  85.3 6.8 %collective-permute-start.18 = (f32[2,64,128]{2,1,0:T(8,128)S(1)}, f32[2,64,128]{2,1,0:T(8,128)S(1)}, u32[]{:S(2)}, u32[]{:S(2)}) collective-permute-start(f32[2,64,128]{2,1,0:T(8,128)S(1)} %fusion.3), channel_id=1, source_target_pairs={{0,16},{4,20},{8,24},{12,28},{16,0},{20,4},{24,8},{28,12},{1,17},{... | collective-permute-start | bytes 196616 | tf_op jit(solution)/shard_map/ppermute | solution.py:513
  92.1 1.4 collective-permute-start.17
  93.5 1.5 %collective-permute-done.18 = f32[2,64,128]{2,1,0:T(8,128)S(1)} collective-permute-done((f32[2,64,128]{2,1,0:T(8,128)S(1)}, f32[2,64,128]{2,1,0:T(8,128)S(1)}, u32[]{:S(2)}, u32[]{:S(2)}) %collective-permute-start.18) | collective-permute-done | bytes 65568 | tf_op jit(solution)/shard_map/ppermute | solution.py:513
  95.0 2.0 %collective-permute-done.17 = f32[2,64,128]{2,1,0:T(8,128)S(1)} collective-permute-done((f32[2,64,128]{2,1,0:T(8,128)S(1)}, f32[2,64,128]{2,1,0:T(8,128)S(1)}, u32[]{:S(2)}, u32[]{:S(2)}) %collective-permute-start.17) | collective-permute-done | bytes 65568 | tf_op jit(solution)/shard_map/ppermute | solution.py:513
  97.0 2.1 %collective-permute-start.23 = (f32[64,128]{1,0:T(8,128)S(1)}, f32[64,128]{1,0:T(8,128)S(1)}, u32[]{:S(2)}, u32[]{:S(2)}) collective-permute-start(f32[64,128]{1,0:T(8,128)S(1)} %get-tuple-element.42), channel_id=1, source_target_pairs={{0,3},{1,2},{2,1},{3,0},{4,7},{5,6},{6,5},{7,4},{8,11},{9,10},{10,... | collective-permute-start | bytes 98312 | tf_op jit(solution)/shard_map/ppermute | solution.py:516
  99.2 2.3 %collective-permute-start.21 = (f32[64,128]{1,0:T(8,128)S(1)}, f32[64,128]{1,0:T(8,128)S(1)}, u32[]{:S(2)}, u32[]{:S(2)}) collective-permute-start(f32[64,128]{1,0:T(8,128)S(1)} %get-tuple-element.42), channel_id=1, source_target_pairs={{0,1},{1,0},{2,3},{3,2},{4,5},{5,4},{6,7},{7,6},{8,9},{9,8},{10,11... | collective-permute-start | bytes 98312 | tf_op jit(solution)/shard_map/ppermute | solution.py:516
  101.7 1.1 collective-permute-done.23
  102.8 1.2 collective-permute-done.22
  104.2 4.7 %factor.1.inverse_ref = f32[128,128]{1,0:T(8,128)S(1)} custom-call(s32[5]{0:T(128)S(1)} %concatenate.12.where_ref, f32[64,128]{1,0:T(8,128)S(1)} %get-tuple-element.41.refs_0_, f32[64,128]{1,0:T(8,128)S(1)} %collective-permute-done.20.refs_1_), custom_call_target="tpu_custom_call" | custom-call | tf_op jit(solution)/shard_map/factor/pallas_call | solution.py:362
  108.9 6.0 %core.1.core_ref = f32[128,128]{1,0:T(8,128)S(1)} custom-call(s32[5]{0:T(128)S(1)} %concatenate.12.where_ref, f32[128,128]{1,0:T(8,128)S(1)} %factor.1.inverse_ref, f32[64,128]{1,0:T(8,128)S(1)} %add_add_fusion.1.refs_0_, f32[64,128]{1,0:T(8,128)S(1)} %collective-permute-done.24.refs_1_), custom_call_target="tpu_custom_call" | custom-call | tf_op jit(solution)/shard_map/core/pallas_call | solution.py:407
  114.9 28.6 %finish.1 = (f32[2048,4096]{1,0:T(8,128)}, bf16[2048,4096]{1,0:T(8,128)(2,1)}) custom-call(s32[18]{0:T(128)S(1)} %concatenate.13.place_ref, f32[4,128,512]{2,1,0:T(8,128)S(1)} %pad_maximum_fusion.left_ref, f32[128,128]{1,0:T(8,128)S(1)} %core.1.core_ref, f32[8,128,512]{2,1,0:T(8,128)S(1)} %bitcast_dynamic-update-slice_fusion.right_ref, ...), custom_call_target="tpu_custom_call" | custom-call | tf_op jit(solution)/shard_map/finish/pallas_call | solution.py:466
  (54 shorter events, 3.0 us)
Async XLA Ops:
  12.8 11.3 %collective-permute-start = (f32[3,128,512]{2,1,0:T(8,128)S(1)}, f32[3,128,512]{2,1,0:T(8,128)S(1)}, u32[]{:S(2)}, u32[]{:S(2)}) collective-permute-start(f32[3,128,512]{2,1,0:T(8,128)S(1)} %get-tuple-element.30), channel_id=1, source_target_pairs={{0,4},{4,0},{8,12},{12,8},{16,20},{20,16},{24,28},{28,24},{1,5},{5... | collective-permute-start | bytes 2359304 | tf_op jit(solution)/shard_map/ppermute | solution.py:509
  24.3 11.8 %collective-permute-start.2 = (f32[128,512]{1,0:T(8,128)S(1)}, f32[128,512]{1,0:T(8,128)S(1)}, u32[]{:S(2)}, u32[]{:S(2)}) collective-permute-start(f32[128,512]{1,0:T(8,128)S(1)} %get-tuple-element.46), channel_id=1, source_target_pairs={{0,8},{4,12},{8,0},{12,4},{16,24},{20,28},{24,16},{28,20},{1,9},{5... | collective-permute-start | bytes 786440 | tf_op jit(solution)/shard_map/ppermute | solution.py:513
  26.8 13.9 %collective-permute-start.4 = (f32[128,512]{1,0:T(8,128)S(1)}, f32[128,512]{1,0:T(8,128)S(1)}, u32[]{:S(2)}, u32[]{:S(2)}) collective-permute-start(f32[128,512]{1,0:T(8,128)S(1)} %get-tuple-element.47), channel_id=1, source_target_pairs={{0,24},{4,28},{8,16},{12,20},{16,8},{20,12},{24,0},{28,4},{1,25},{... | collective-permute-start | bytes 786440 | tf_op jit(solution)/shard_map/ppermute | solution.py:513
  28.3 13.8 %collective-permute-start.3 = (f32[128,512]{1,0:T(8,128)S(1)}, f32[128,512]{1,0:T(8,128)S(1)}, u32[]{:S(2)}, u32[]{:S(2)}) collective-permute-start(f32[128,512]{1,0:T(8,128)S(1)} %get-tuple-element.48), channel_id=1, source_target_pairs={{0,16},{4,20},{8,24},{12,28},{16,0},{20,4},{24,8},{28,12},{1,17},{... | collective-permute-start | bytes 786440 | tf_op jit(solution)/shard_map/ppermute | solution.py:513
  36.0 6.0 %collective-permute-start.1 = (f32[128,512]{1,0:T(8,128)S(1)}, f32[128,512]{1,0:T(8,128)S(1)}, u32[]{:S(2)}, u32[]{:S(2)}) collective-permute-start(f32[128,512]{1,0:T(8,128)S(1)} %slice_bitcast_fusion.3), channel_id=1, source_target_pairs={{0,4},{4,0},{8,12},{12,8},{16,20},{20,16},{24,28},{28,24},{1,5},{5... | collective-permute-start | bytes 786440 | tf_op jit(solution)/shard_map/ppermute | solution.py:509
  42.2 7.3 %collective-permute-start.6 = (f32[128,512]{1,0:T(8,128)S(1)}, f32[128,512]{1,0:T(8,128)S(1)}, u32[]{:S(2)}, u32[]{:S(2)}) collective-permute-start(f32[128,512]{1,0:T(8,128)S(1)} %fusion.2.refs_5_.refs_0_), channel_id=1, source_target_pairs={{0,16},{4,20},{8,24},{12,28},{16,0},{20,4},{24,8},{28,12},{1,17},{... | collective-permute-start | bytes 786440 | tf_op jit(solution)/shard_map/ppermute | solution.py:513
  42.6 7.3 %collective-permute-start.5 = (f32[128,512]{1,0:T(8,128)S(1)}, f32[128,512]{1,0:T(8,128)S(1)}, u32[]{:S(2)}, u32[]{:S(2)}) collective-permute-start(f32[128,512]{1,0:T(8,128)S(1)} %fusion.2.refs_5_.refs_0_), channel_id=1, source_target_pairs={{0,8},{4,12},{8,0},{12,4},{16,24},{20,28},{24,16},{28,20},{1,9},{5... | collective-permute-start | bytes 786440 | tf_op jit(solution)/shard_map/ppermute | solution.py:513
  44.3 12.5 %collective-permute-start.15 = (f32[128,512]{1,0:T(8,128)S(1)}, f32[128,512]{1,0:T(8,128)S(1)}, u32[]{:S(2)}, u32[]{:S(2)}) collective-permute-start(f32[128,512]{1,0:T(8,128)S(1)} %fusion.2.refs_5_.refs_0_), channel_id=1, source_target_pairs={{0,4},{4,0},{8,12},{12,8},{16,20},{20,16},{24,28},{28,24},{1,5},{5... | collective-permute-start | bytes 786440 | tf_op jit(solution)/shard_map/ppermute | solution.py:509
  49.5 10.0 %collective-permute-start.13 = (f32[128,512]{1,0:T(8,128)S(1)}, f32[128,512]{1,0:T(8,128)S(1)}, u32[]{:S(2)}, u32[]{:S(2)}) collective-permute-start(f32[128,512]{1,0:T(8,128)S(1)} %collective-permute-done.6.refs_3_.refs_2_), channel_id=1, source_target_pairs={{0,4},{4,0},{8,12},{12,8},{16,20},{20,16},{24,28},{28,24},{1,5},{5... | collective-permute-start | bytes 786440 | tf_op jit(solution)/shard_map/ppermute | solution.py:509
  49.9 12.3 %collective-permute-start.12 = (f32[128,512]{1,0:T(8,128)S(1)}, f32[128,512]{1,0:T(8,128)S(1)}, u32[]{:S(2)}, u32[]{:S(2)}) collective-permute-start(f32[128,512]{1,0:T(8,128)S(1)} %collective-permute-done.5.refs_2_.refs_1_), channel_id=1, source_target_pairs={{0,4},{4,0},{8,12},{12,8},{16,20},{20,16},{24,28},{28,24},{1,5},{5... | collective-permute-start | bytes 786440 | tf_op jit(solution)/shard_map/ppermute | solution.py:509
  50.0 13.0 %collective-permute-start.7 = (f32[128,512]{1,0:T(8,128)S(1)}, f32[128,512]{1,0:T(8,128)S(1)}, u32[]{:S(2)}, u32[]{:S(2)}) collective-permute-start(f32[128,512]{1,0:T(8,128)S(1)} %collective-permute-done.5.refs_2_.refs_1_), channel_id=1, source_target_pairs={{0,16},{4,20},{8,24},{12,28},{16,0},{20,4},{24,8},{28,12},{1,17},{... | collective-permute-start | bytes 786440 | tf_op jit(solution)/shard_map/ppermute | solution.py:513
  51.3 16.7 %collective-permute-start.11 = (f32[128,512]{1,0:T(8,128)S(1)}, f32[128,512]{1,0:T(8,128)S(1)}, u32[]{:S(2)}, u32[]{:S(2)}) collective-permute-start(f32[128,512]{1,0:T(8,128)S(1)} %fusion.2.refs_5_.refs_0_), channel_id=1, source_target_pairs={{0,3},{1,11},{2,19},{4,7},{5,15},{6,23},{8,2},{9,10},{11,26},{12,6... | collective-permute-start | bytes 786440 | tf_op jit(solution)/shard_map/ppermute | solution.py:577
  56.8 12.4 %collective-permute-start.10 = (f32[128,512]{1,0:T(8,128)S(1)}, f32[128,512]{1,0:T(8,128)S(1)}, u32[]{:S(2)}, u32[]{:S(2)}) collective-permute-start(f32[128,512]{1,0:T(8,128)S(1)} %fusion.2.refs_5_.refs_0_), channel_id=1, source_target_pairs={{0,2},{1,10},{3,26},{4,6},{5,14},{7,30},{8,3},{9,11},{10,19},{12,7... | collective-permute-start | bytes 786440 | tf_op jit(solution)/shard_map/ppermute | solution.py:577
  59.5 14.5 %collective-permute-start.9 = (f32[128,512]{1,0:T(8,128)S(1)}, f32[128,512]{1,0:T(8,128)S(1)}, u32[]{:S(2)}, u32[]{:S(2)}) collective-permute-start(f32[128,512]{1,0:T(8,128)S(1)} %fusion.2.refs_5_.refs_0_), channel_id=1, source_target_pairs={{0,1},{2,17},{3,25},{4,5},{6,21},{7,29},{9,8},{10,16},{11,24},{13,... | collective-permute-start | bytes 786440 | tf_op jit(solution)/shard_map/ppermute | solution.py:577
  62.1 11.9 %collective-permute-start.8 = (f32[128,512]{1,0:T(8,128)S(1)}, f32[128,512]{1,0:T(8,128)S(1)}, u32[]{:S(2)}, u32[]{:S(2)}) collective-permute-start(f32[128,512]{1,0:T(8,128)S(1)} %fusion.2.refs_5_.refs_0_), channel_id=1, source_target_pairs={{1,8},{2,16},{3,24},{5,12},{6,20},{7,28},{8,1},{10,17},{11,25},{12... | collective-permute-start | bytes 786440 | tf_op jit(solution)/shard_map/ppermute | solution.py:577
  63.0 2.5 %collective-permute-start.14 = (f32[128,512]{1,0:T(8,128)S(1)}, f32[128,512]{1,0:T(8,128)S(1)}, u32[]{:S(2)}, u32[]{:S(2)}) collective-permute-start(f32[128,512]{1,0:T(8,128)S(1)} %collective-permute-done.7.refs_4_.refs_3_), channel_id=1, source_target_pairs={{0,4},{4,0},{8,12},{12,8},{16,20},{20,16},{24,28},{28,24},{1,5},{5... | collective-permute-start | bytes 786440 | tf_op jit(solution)/shard_map/ppermute | solution.py:509
  75.6 1.3 collective-permute-start.16
  76.9 16.6 %collective-permute-start.19 = (f32[2,64,128]{2,1,0:T(8,128)S(1)}, f32[2,64,128]{2,1,0:T(8,128)S(1)}, u32[]{:S(2)}, u32[]{:S(2)}) collective-permute-start(f32[2,64,128]{2,1,0:T(8,128)S(1)} %fusion.3), channel_id=1, source_target_pairs={{0,24},{4,28},{8,16},{12,20},{16,8},{20,12},{24,0},{28,4},{1,25},{... | collective-permute-start | bytes 196616 | tf_op jit(solution)/shard_map/ppermute | solution.py:513
  85.3 9.7 %collective-permute-start.18 = (f32[2,64,128]{2,1,0:T(8,128)S(1)}, f32[2,64,128]{2,1,0:T(8,128)S(1)}, u32[]{:S(2)}, u32[]{:S(2)}) collective-permute-start(f32[2,64,128]{2,1,0:T(8,128)S(1)} %fusion.3), channel_id=1, source_target_pairs={{0,16},{4,20},{8,24},{12,28},{16,0},{20,4},{24,8},{28,12},{1,17},{... | collective-permute-start | bytes 196616 | tf_op jit(solution)/shard_map/ppermute | solution.py:513
  92.1 4.9 %collective-permute-start.17 = (f32[2,64,128]{2,1,0:T(8,128)S(1)}, f32[2,64,128]{2,1,0:T(8,128)S(1)}, u32[]{:S(2)}, u32[]{:S(2)}) collective-permute-start(f32[2,64,128]{2,1,0:T(8,128)S(1)} %fusion.3), channel_id=1, source_target_pairs={{0,8},{4,12},{8,0},{12,4},{16,24},{20,28},{24,16},{28,20},{1,9},{5... | collective-permute-start | bytes 196616 | tf_op jit(solution)/shard_map/ppermute | solution.py:513
  97.0 5.8 %collective-permute-start.23 = (f32[64,128]{1,0:T(8,128)S(1)}, f32[64,128]{1,0:T(8,128)S(1)}, u32[]{:S(2)}, u32[]{:S(2)}) collective-permute-start(f32[64,128]{1,0:T(8,128)S(1)} %get-tuple-element.42), channel_id=1, source_target_pairs={{0,3},{1,2},{2,1},{3,0},{4,7},{5,6},{6,5},{7,4},{8,11},{9,10},{10,... | collective-permute-start | bytes 98312 | tf_op jit(solution)/shard_map/ppermute | solution.py:516
  99.2 4.8 %collective-permute-start.22 = (f32[64,128]{1,0:T(8,128)S(1)}, f32[64,128]{1,0:T(8,128)S(1)}, u32[]{:S(2)}, u32[]{:S(2)}) collective-permute-start(f32[64,128]{1,0:T(8,128)S(1)} %get-tuple-element.42), channel_id=1, source_target_pairs={{0,2},{1,3},{2,0},{3,1},{4,6},{5,7},{6,4},{7,5},{8,10},{9,11},{10,... | collective-permute-start | bytes 98312 | tf_op jit(solution)/shard_map/ppermute | solution.py:516
  99.2 4.8 %collective-permute-start.21 = (f32[64,128]{1,0:T(8,128)S(1)}, f32[64,128]{1,0:T(8,128)S(1)}, u32[]{:S(2)}, u32[]{:S(2)}) collective-permute-start(f32[64,128]{1,0:T(8,128)S(1)} %get-tuple-element.42), channel_id=1, source_target_pairs={{0,1},{1,0},{2,3},{3,2},{4,5},{5,4},{6,7},{7,6},{8,9},{9,8},{10,11... | collective-permute-start | bytes 98312 | tf_op jit(solution)/shard_map/ppermute | solution.py:516
  101.5 2.7 %collective-permute-start.20 = (f32[64,128]{1,0:T(8,128)S(1)}, f32[64,128]{1,0:T(8,128)S(1)}, u32[]{:S(2)}, u32[]{:S(2)}) collective-permute-start(f32[64,128]{1,0:T(8,128)S(1)} %get-tuple-element.41.refs_0_), channel_id=1, source_target_pairs={{0,4},{4,0},{8,12},{12,8},{16,20},{20,16},{24,28},{28,24},{1,5},{5... | collective-permute-start | bytes 98312 | tf_op jit(solution)/shard_map/ppermute | solution.py:509
  104.0 4.9 %collective-permute-start.24 = (f32[64,128]{1,0:T(8,128)S(1)}, f32[64,128]{1,0:T(8,128)S(1)}, u32[]{:S(2)}, u32[]{:S(2)}) collective-permute-start(f32[64,128]{1,0:T(8,128)S(1)} %add_add_fusion.1.refs_0_), channel_id=1, source_target_pairs={{0,4},{4,0},{8,12},{12,8},{16,20},{20,16},{24,28},{28,24},{1,5},{5... | collective-permute-start | bytes 98312 | tf_op jit(solution)/shard_map/ppermute | solution.py:509
